TPU v7x, 32 devices: a whole 2x2x4 slice. The times are simulated.
32 devices in a mesh: wide: 8 (over z, y), narrow: 4 (over x, core).
Axes of the slice: x: 2, y: 2, z: 4, core: 2. Of those that a mesh axis runs over, the one named last changes fastest.
Arguments:
- targets: float32 [32768, 64], P(('wide', 'narrow')), may hold values from -6 to 6
- train_features: bfloat16 [32768, 128], P(('wide', 'narrow')), may hold values from -6 to 6
- test_features: bfloat16 [1024, 128], P(('wide', 'narrow')), may hold values from -6 to 6
- left_factors: float32 [32768, 4, 128], P(('wide', 'narrow')), may hold values from -0.5 to 0.5
- right_factors: float32 [32768, 4, 128], P(('wide', 'narrow')), may hold values from -0.03125 to 0.03125
- capacitance: float32 [15, 256, 256], replicated, may hold values from -0.375 to 0.375
- pivots: int32 [15, 256], replicated, may hold values from 0 to 255, each once within a row
Outputs:
- solved_targets: float32 [32768, 64], P(('wide', 'narrow'))
- predictions: float32 [1024, 64], P(('wide', 'narrow'))
Inputs may be any that keep to these rules, and one draw needn't show every extreme that they name: `pivots`: each row is a permutation of 0 .. 255.
All inputs are finite; a program needn't handle non-finite values.
Results may differ from a plain program's by a relative error of at most 0.0049.
Values may be sent and summed in bfloat16 or wider, within the bound.
A program may use at most 128 MiB of HBM per device.

v0:
```python
import functools

import jax
import jax.numpy as jnp
from jax import lax
from jax.experimental import pallas as pl
from jax.experimental.pallas import tpu as pltpu
from jax.sharding import PartitionSpec as P

LEVELS = 4
spread_coef = 3.0
MESH = pl.DeviceIdType.MESH
HIGHEST = lax.Precision.HIGHEST


def dot(a, b, precision=None):
    return jnp.dot(a, b, precision=precision, preferred_element_type=jnp.float32)


def dot_nt(a, b, precision=None):
    return lax.dot_general(
        a, b, (((1,), (1,)), ((), ())), precision=precision, preferred_element_type=jnp.float32
    )


def split(value):
    high = value.astype(jnp.bfloat16)
    return high, (value - high.astype(jnp.float32)).astype(jnp.bfloat16)


def g_row(level, k, rank):
    return ((level - 1) * (level - 2) // 2 + (k - 1)) * rank


def kernel(
    n_dev, narrow,
    targets_h, train_h, test_h, left_h, right_h, cap_h, piv_ref,
    cur_ref, pred_ref,
    tgt, train, left, right, cap, gath, lsplit, mt, kmat,
    acc_t, acc_g, par_t, par_g, send_t, send_g, recv_t, recv_g,
    share, term_f, term_b, term_in,
    load_sem, cap_sem, t1_send, t1_recv, tt_send, tt_recv, gg_send, gg_recv,
    ag_send, ag_recv, fw_send, fw_recv, rs_send, rs_recv,
):
    bits = n_dev.bit_length() - 1
    pos = lax.axis_index("wide") * narrow + lax.axis_index("narrow")
    points, width = tgt.shape
    rank = right.shape[2]
    feat = train.shape[1]
    rows = test_h.shape[0]
    half = rows // 2
    parity = pos % 2
    slot = pos // 2
    pairs = n_dev // 2

    def coords(dev):
        return (dev // narrow, dev % narrow)

    barrier = pltpu.get_barrier_semaphore()

    def greet(k, carry):
        pl.semaphore_signal(
            barrier, inc=1, device_id=coords((pos + k) % n_dev), device_id_type=MESH
        )
        return carry

    lax.fori_loop(1, n_dev, greet, 0)

    own_test = gath.at[parity, pl.ds(pl.multiple_of(slot * rows, rows), rows)]
    loads = [
        pltpu.make_async_copy(targets_h, tgt, load_sem.at[0]),
        pltpu.make_async_copy(train_h, train, load_sem.at[1]),
        pltpu.make_async_copy(test_h, own_test, load_sem.at[2]),
    ]
    for lev in range(LEVELS):
        loads.append(pltpu.make_async_copy(right_h.at[:, lev, :], right.at[lev], load_sem.at[3 + lev]))
        loads.append(
            pltpu.make_async_copy(left_h.at[:, lev, :], left.at[lev], load_sem.at[3 + LEVELS + lev])
        )
    caps = []
    odds, heaps = [], []
    for level in range(1, LEVELS + 1):
        child = pos // (n_dev >> level)
        odds.append(child % 2)
        heaps.append((1 << level - 1) - 1 + child // 2)
        caps.append(
            pltpu.make_async_copy(
                cap_h.at[heaps[-1], pl.ds(pl.multiple_of(odds[-1] * rank, rank), rank)],
                cap.at[level - 1],
                cap_sem.at[level - 1],
            )
        )
    for copy in loads + caps:
        copy.start()
    for copy in loads:
        copy.wait()

    tgt_high, tgt_low = split(tgt[...].T)
    stack = [tgt_high, tgt_low]
    for lev in range(LEVELS - 1):
        stack.append(left[lev].T.astype(jnp.bfloat16))
    for level in range(1, LEVELS + 1):
        right_high, right_low = split(right[level - 1])
        product = dot(jnp.concatenate(stack[: 1 + level], axis=0), right_high)
        acc_t[pl.ds((level - 1) * width, width)] = (
            product[:width] + product[width : 2 * width] + dot(tgt_high, right_low)
        )
        if level > 1:
            acc_g[pl.ds(g_row(level, 1, rank), (level - 1) * rank)] = product[2 * width :]

    def partner_of(bit):
        mask = 1 << bit
        return coords(pos + mask * (1 - 2 * ((pos // mask) % 2)))

    def levels_at(bit):
        return min(LEVELS, bits - bit)

    def t1_copy(bit):
        part = pl.ds(0, width)
        return pltpu.make_async_remote_copy(
            src_ref=send_t.at[bit, part], dst_ref=recv_t.at[bit, part],
            send_sem=t1_send.at[bit], recv_sem=t1_recv.at[bit],
            device_id=partner_of(bit), device_id_type=MESH,
        )

    def tt_copy(bit):
        part = pl.ds(width, (levels_at(bit) - 1) * width)
        return pltpu.make_async_remote_copy(
            src_ref=send_t.at[bit, part], dst_ref=recv_t.at[bit, part],
            send_sem=tt_send.at[bit], recv_sem=tt_recv.at[bit],
            device_id=partner_of(bit), device_id_type=MESH,
        )

    def gg_copy(bit):
        part = pl.ds(0, g_row(levels_at(bit) + 1, 1, rank))
        return pltpu.make_async_remote_copy(
            src_ref=send_g.at[bit, part], dst_ref=recv_g.at[bit, part],
            send_sem=gg_send.at[bit], recv_sem=gg_recv.at[bit],
            device_id=partner_of(bit), device_id_type=MESH,
        )

    def send_first(bit):
        part = pl.ds(0, width)
        send_t[bit, part] = acc_t[part]
        t1_copy(bit).start()

    def send_rest(bit):
        if levels_at(bit) > 1:
            part = pl.ds(width, (levels_at(bit) - 1) * width)
            send_t[bit, part] = acc_t[part]
            tt_copy(bit).start()
            part = pl.ds(0, g_row(levels_at(bit) + 1, 1, rank))
            send_g[bit, part] = acc_g[part].astype(jnp.bfloat16)
            gg_copy(bit).start()

    def take_first(bit):
        t1_copy(bit).wait()
        part = pl.ds(0, width)
        if bit < bits - 1:
            acc_t[part] = acc_t[part] + recv_t[bit, part]
        else:
            par_t[part] = recv_t[bit, part]

    def take_rest(bit):
        if levels_at(bit) == 1:
            return
        tt_copy(bit).wait()
        gg_copy(bit).wait()
        top = bits - bit
        summed = min(LEVELS, top - 1)
        if summed > 1:
            part = pl.ds(width, (summed - 1) * width)
            acc_t[part] = acc_t[part] + recv_t[bit, part]
            part = pl.ds(0, g_row(summed + 1, 1, rank))
            acc_g[part] = acc_g[part] + recv_g[bit, part].astype(jnp.float32)
        if top <= LEVELS:
            part = pl.ds((top - 1) * width, width)
            par_t[part] = recv_t[bit, part]
            part = pl.ds(g_row(top, 1, rank), (top - 1) * rank)
            par_g[part] = recv_g[bit, part].astype(jnp.float32)

    pl.semaphore_wait(barrier, n_dev - 1)
    send_first(0)
    send_rest(0)

    def spread(k, carry):
        dev = (pos + 2 * k) % n_dev
        pltpu.make_async_remote_copy(
            src_ref=own_test, dst_ref=own_test, send_sem=ag_send, recv_sem=ag_recv,
            device_id=coords(dev), device_id_type=MESH,
        ).start()
        return carry

    lax.fori_loop(1, pairs, spread, 0)

    for copy in caps:
        copy.wait()
    order = lax.broadcasted_iota(jnp.int32, (2 * rank, 2 * rank), 0)

    def pivot(lev):
        chosen = (order == piv_ref[pl.ds(heaps[lev], 1), :]).astype(jnp.float32)
        mt[lev] = dot_nt(chosen, cap[lev], HIGHEST)

    def halves(lev):
        high, low = split(left[lev])
        lsplit[0, :, pl.ds(lev * rank, rank)] = high
        lsplit[1, :, pl.ds(lev * rank, rank)] = low

    take_first(0)
    send_first(1)
    take_rest(0)
    send_rest(1)
    for lev in range(LEVELS):
        pivot(lev)

    def forward(which):
        part = gath.at[which]
        return pltpu.make_async_remote_copy(
            src_ref=part, dst_ref=part, send_sem=fw_send, recv_sem=fw_recv,
            device_id=partner_of(0), device_id_type=MESH,
        )

    def drain(ref, count, sem):
        part = ref.at[pl.ds(0, count)]
        pltpu.make_async_copy(part, part, sem).wait()

    scale = spread_coef / feat
    chunk = 128

    def kernel_rows(which):
        train_bf = train[...]
        train_f = train_bf.astype(jnp.float32)
        ones = jnp.ones((8, feat), jnp.float32)
        train_sq = dot_nt(ones, train_f * train_f, HIGHEST)[:1]

        def step(i, carry):
            part = pl.ds(pl.multiple_of(i * chunk, chunk), chunk)
            some = gath[which, part]
            some_f = some.astype(jnp.float32)
            some_sq = jnp.sum(some_f * some_f, axis=1, keepdims=True)
            dist = some_sq + train_sq - 2.0 * dot_nt(some, train_bf)
            kmat[which, part] = jnp.exp(-scale * dist).astype(jnp.bfloat16)
            return carry

        lax.fori_loop(0, pairs * rows // chunk, step, 0)

    for bit in range(1, bits):
        take_first(bit)
        if bit < bits - 1:
            send_first(bit + 1)
        if bit > 1:
            take_rest(bit - 1)
            send_rest(bit)
        if bit == 1:
            for lev in range(LEVELS):
                halves(lev)
        if bit == bits - 3:
            drain(gath.at[0], (pairs - 1) * rows, ag_recv)
            forward(parity).start()
            kernel_rows(parity)
        if bit == bits - 2:
            forward(parity).wait()
            kernel_rows(1 - parity)

    shares = []
    for level in range(1, LEVELS + 1):
        if level == 2 and bits > 1:
            take_rest(bits - 1)
        t_part = pl.ds((level - 1) * width, width)
        mine, other = acc_t[t_part], par_t[t_part]
        for k in range(1, level):
            g_part = pl.ds(g_row(level, k, rank), rank)
            mine = mine - dot(shares[k - 1], acc_g[g_part], HIGHEST)
            other = other - dot(shares[k - 1], par_g[g_part], HIGHEST)
        odd = odds[level - 1]
        at_mine = pl.ds(pl.multiple_of((1 - odd) * rank, rank), rank)
        at_other = pl.ds(pl.multiple_of(odd * rank, rank), rank)
        shares.append(
            dot(mine, mt[level - 1, at_mine], HIGHEST) + dot(other, mt[level - 1, at_other], HIGHEST)
        )
    share_high, share_low = split(jnp.concatenate(shares, axis=1))
    current = tgt[...] - (
        dot_nt(lsplit[0], share_high) + dot_nt(lsplit[1], share_high) + dot_nt(lsplit[0], share_low)
    )
    cur_ref[...] = current
    weights = current.astype(jnp.bfloat16)

    big = min(512, pairs * rows)
    for which in range(2):

        def weigh(i, carry, which=which):
            part = pl.ds(pl.multiple_of(i * big, big), big)
            terms = dot(kmat[which, part], weights).reshape(big // rows, 2, half, width)
            packed = jnp.concatenate(
                [terms[:, 0].reshape(big // 2, width), terms[:, 1].reshape(big // 2, width)], axis=1
            )
            term_b[which, pl.ds(pl.multiple_of(i * (big // 2), big // 2), big // 2)] = packed.astype(
                jnp.bfloat16
            )
            return carry

        lax.fori_loop(0, pairs * rows // big, weigh, 0)

    def scatter(k, carry):
        dev = (pos + k) % n_dev
        pltpu.make_async_remote_copy(
            src_ref=term_b.at[dev % 2, pl.ds(pl.multiple_of(dev // 2 * half, half), half)],
            dst_ref=term_in.at[pl.ds(pl.multiple_of((k - 1) * half, half), half)],
            send_sem=rs_send, recv_sem=rs_recv, device_id=coords(dev), device_id_type=MESH,
        ).start()
        return carry

    lax.fori_loop(1, n_dev, scatter, 0)
    drain(gath.at[0], (pairs - 1) * rows, ag_send)
    drain(term_in, (n_dev - 1) * half, rs_recv)
    total = term_b[parity, pl.ds(pl.multiple_of(slot * half, half), half)].astype(jnp.float32)
    arrived = term_in[...].astype(jnp.float32).reshape(n_dev - 1, half, 2 * width)
    total = total + jnp.sum(arrived, axis=0)
    pred_ref[pl.ds(0, half)] = total[:, :width]
    pred_ref[pl.ds(half, half)] = total[:, width:]
    drain(term_in, (n_dev - 1) * half, rs_send)


def body(n_dev, narrow, targets, train, test, left, right, cap, pivots):
    points, width = targets.shape
    rank = left.shape[2]
    feat = train.shape[1]
    rows = test.shape[0]
    bits = n_dev.bit_length() - 1
    pairs = n_dev // 2
    g_rows = g_row(LEVELS + 1, 1, rank)
    t_rows = LEVELS * width
    f32, bf16 = jnp.float32, jnp.bfloat16
    vmem = pltpu.VMEM
    dma = pltpu.SemaphoreType.DMA
    hbm_spec = pl.BlockSpec(memory_space=pl.ANY)
    vmem_spec = pl.BlockSpec(memory_space=pltpu.VMEM)
    return pl.pallas_call(
        functools.partial(kernel, n_dev, narrow),
        out_shape=(
            jax.ShapeDtypeStruct((points, width), f32),
            jax.ShapeDtypeStruct((rows, width), f32),
        ),
        in_specs=[hbm_spec] * 6 + [vmem_spec],
        out_specs=(vmem_spec, vmem_spec),
        scratch_shapes=[
            vmem((points, width), f32),
            vmem((points, feat), bf16),
            vmem((LEVELS, points, rank), f32),
            vmem((LEVELS, points, rank), f32),
            vmem((LEVELS, rank, 2 * rank), f32),
            vmem((2, pairs * rows, feat), bf16),
            vmem((2, points, LEVELS * rank), bf16),
            vmem((LEVELS, 2 * rank, rank), f32),
            vmem((2, pairs * rows, points), bf16),
            vmem((t_rows, rank), f32),
            vmem((g_rows, rank), f32),
            vmem((t_rows, rank), f32),
            vmem((g_rows, rank), f32),
            vmem((bits, t_rows, rank), f32),
            vmem((bits, g_rows, rank), bf16),
            vmem((bits, t_rows, rank), f32),
            vmem((bits, g_rows, rank), bf16),
            vmem((8, 128), f32),
            vmem((8, 128), f32),
            vmem((2, pairs * rows // 2, 2 * width), bf16),
            vmem(((n_dev - 1) * rows // 2, 2 * width), bf16),
            dma((3 + 2 * LEVELS,)),
            dma((LEVELS,)),
            dma((bits,)), dma((bits,)), dma((bits,)), dma((bits,)), dma((bits,)), dma((bits,)),
            dma, dma, dma, dma, dma, dma,
        ],
        compiler_params=pltpu.CompilerParams(
            collective_id=0, has_side_effects=True, vmem_limit_bytes=60 * 1024 * 1024
        ),
    )(targets, train, test, left, right, cap, pivots)


def solution(mesh):
    both = ("wide", "narrow")
    placed = (
        P(both, None), P(both, None), P(both, None),
        P(both, None, None), P(both, None, None), P(), P(),
    )
    sizes = dict(mesh.shape)
    return jax.shard_map(
        functools.partial(body, sizes["wide"] * sizes["narrow"], sizes["narrow"]),
        mesh=mesh,
        in_specs=placed,
        out_specs=(P(both, None), P(both, None)),
        check_vma=False,
    )
```

profile of v0, /device:TPU:0, one launch (start us, length us, event | category | flops | bytes accessed | tf_op | source)
XLA Modules:
  0.0 43.5 jit_solution(17687733554478837456)
XLA Ops:
  0.6 1.9 %copy.9.targets_h = f32[1024,64]{1,0:T(8,128)} copy(f32[1024,64]{0,1:T(8,128)} %param.7) | data formatting | bytes 524288 | tf_op args[0]
  2.6 37.6 %shard_map.86 = (f32[1024,64]{1,0:T(8,128)}, f32[32,64]{1,0:T(8,128)}) custom-call(f32[1024,64]{1,0:T(8,128)} %copy.9.targets_h, bf16[1024,128]{1,0:T(8,128)(2,1)} %train_h.1, bf16[32,128]{1,0:T(8,128)(2,1)} %test_h.1, f32[1024,4,128]{2,1,0:T(4,128)} %left_h.1, f32[1024,4,128]{2,1,0:T(4,128)} %right_h.1, f32[15,256,256]{2,1,0:T(8,128)} %cap_h.1, ...), custom_call_target="tpu_custom_call" | custom-call | tf_op jit(solution)/shard_map/pallas_call | solution.py:338
  40.2 1.9 %copy.10 = f32[1024,64]{0,1:T(8,128)} copy(f32[1024,64]{1,0:T(8,128)} %get-tuple-element.2) | data formatting | bytes 524288 | tf_op jit(solution)/shard_map/pallas_call | solution.py:338
  42.1 1.3 %copy.12 = f32[32,64]{1,0:T(8,128)} copy(f32[32,64]{1,0:T(8,128)} %get-tuple-element.7) | data formatting | bytes 16384
where the time goes:
time: 43.8 us; the launch traced here: 43.5 us
  Pallas kernels  37.6 us (86%)
  local copies, waits for them, and re-layouts  5.19 us (12%)
  between operations  0.64 us (1%)
    pallas_call x1, Pallas kernels, body(): pl.pallas_call(functools.partial(kernel, n_dev, narrow), out_shape=(jax.S...  37.6 us
    unnamed x2, local copies, waits for them, and re-layouts  3.26 us
    pallas_call x1, local copies, waits for them, and re-layouts, body(): pl.pallas_call(functools.partial(kernel, n_dev, narrow), out_shape=(jax.S...  1.93 us

commit v1 on v0

v1 whole, which is shorter than its diff:
```python
import functools
import math
import types

import jax
import jax.numpy as jnp
from jax import lax
from jax.experimental import pallas as pl
from jax.experimental.pallas import tpu as pltpu
from jax.sharding import PartitionSpec as P

LEVELS = 4
OCTET = 8
spread_coef = 3.0
MESH = pl.DeviceIdType.MESH
f32, bf16 = jnp.float32, jnp.bfloat16


def dot(a, b):
    return jnp.dot(a, b, preferred_element_type=f32)


def dot_nt(a, b):
    return lax.dot_general(a, b, (((1,), (1,)), ((), ())), preferred_element_type=f32)


def split(value):
    high = value.astype(bf16)
    return high, (value - high.astype(f32)).astype(bf16)


def halves_of(value):
    high = value.astype(bf16).astype(f32)
    return high, value - high


def group_of(n_dev, level):
    node = n_dev >> (level - 1)
    size = min(OCTET, node)
    return size, node // size


def kernel(n_dev, narrow, names, *refs):
    r = types.SimpleNamespace(**dict(zip(names, refs)))
    pos = lax.axis_index("wide") * narrow + lax.axis_index("narrow")
    width, points = r.tgt.shape
    rank = r.right.shape[2]
    feat = r.train.shape[2]
    rows = r.test_h.shape[0]
    half = rows // 2
    pairs = n_dev // 2
    parity = pos % 2
    slot = pos // 2
    own_rows = pl.ds(pl.multiple_of(slot * half, half), half)

    def coords(dev):
        return (dev // narrow, dev % narrow)

    def flip(mask):
        dev = pos
        for bit in range(mask.bit_length()):
            if mask >> bit & 1:
                dev = dev + (1 << bit) * (1 - 2 * ((pos // (1 << bit)) % 2))
        return coords(dev)

    def remote(src, dst, send_sem, recv_sem, where):
        pltpu.make_async_remote_copy(
            src_ref=src, dst_ref=dst, send_sem=send_sem, recv_sem=recv_sem,
            device_id=where, device_id_type=MESH,
        ).start()

    def drain(part, sem):
        pltpu.make_async_copy(part, part, sem).wait()

    def load(src, dst, sem):
        copy = pltpu.make_async_copy(src, dst, sem)
        copy.start()
        return copy

    test_loads = [
        load(r.test_h.at[pl.ds(h * half, half)], r.gath.at[h, own_rows], r.load_sem.at[0 + h])
        for h in range(2)
    ]
    tgt_load = load(r.tgt_h, r.tgt, r.load_sem.at[2])
    right_loads, left_loads = [], []
    train_load = None
    for lev in range(LEVELS):
        right_loads.append(load(r.right_h.at[:, lev, :], r.right.at[lev], r.load_sem.at[4 + lev]))
        if lev == 0:
            train_load = load(r.train_h, r.train.at[0], r.load_sem.at[3])
        left_loads.append(
            load(r.left_h.at[:, lev, :], r.left.at[lev], r.load_sem.at[4 + LEVELS + lev])
        )
    cap_loads, odds, heaps = [], [], []
    for level in range(1, LEVELS + 1):
        child = pos // (n_dev >> level)
        odd = child % 2
        odds.append(odd)
        heaps.append((1 << level - 1) - 1 + child // 2)
        cap_loads.append([
            load(
                r.cap_h.at[heaps[-1], pl.ds(pl.multiple_of(which * rank, rank), rank)],
                r.cap.at[level - 1, pl.ds(at * rank, rank)],
                r.cap_sem.at[level - 1, at],
            )
            for at, which in enumerate((odd, 1 - odd))
        ])

    barrier = pltpu.get_barrier_semaphore()

    def greet(k, carry):
        pl.semaphore_signal(
            barrier, inc=1, device_id=coords((pos + 2 * k) % n_dev), device_id_type=MESH
        )
        return carry

    lax.fori_loop(1, pairs, greet, 0)
    crossing = range(1, OCTET, 2)
    for k in crossing:
        pl.semaphore_signal(barrier, inc=1, device_id=flip(k), device_id_type=MESH)
    pl.semaphore_wait(barrier, pairs - 1 + len(crossing))

    for copy in test_loads:
        copy.wait()
    own_test = r.gath.at[:, own_rows]

    def spread(k, carry):
        remote(own_test, own_test, r.ag_send, r.ag_recv, coords((pos + 2 * k) % n_dev))
        return carry

    lax.fori_loop(1, pairs, spread, 0)

    def first_send(level):
        size, _ = group_of(n_dev, level)
        mine = pos % size
        lev = level - 1
        for k in range(1, size):
            to = mine
            for bit in range(k.bit_length()):
                if k >> bit & 1:
                    to = to + (1 << bit) * (1 - 2 * ((mine // (1 << bit)) % 2))
            remote(
                getattr(r, f"send{level}").at[to], getattr(r, f"recv{level}").at[k],
                r.p1_send.at[lev], r.p1_recv.at[lev], flip(k),
            )

    def gram(level):
        lev = level - 1
        size, _ = group_of(n_dev, level)
        right_loads[lev].wait()
        high, low = split(r.right[lev])
        product = dot(r.stack[pl.ds(0, 2 * width + lev * rank)], high)
        t = product[:width] + product[width : 2 * width] + dot(r.stack[pl.ds(0, width)], low)
        t_high, t_low = halves_of(t)
        part = width // size
        both = jnp.concatenate(
            [t_high.reshape(size, part, rank), t_low.reshape(size, part, rank)], axis=1
        )
        send = getattr(r, f"send{level}")
        send[:, pl.ds(0, 2 * part)] = both.astype(bf16)
        cut = rank // size
        for k in range(lev):
            piece = product[2 * width + k * rank : 2 * width + (k + 1) * rank]
            send[:, pl.ds(2 * part + k * cut, cut)] = piece.astype(bf16).reshape(size, cut, rank)
        first_send(level)

    def turn(lev):
        left_loads[lev].wait()
        high, low = split(r.left[lev].T)
        r.stack[pl.ds(2 * width + lev * rank, rank)] = high
        r.ltl[pl.ds(lev * rank, rank)] = low

    sums = {}

    def joined(value, level):
        part = width // group_of(n_dev, level)[0]
        top = value[:part] + value[part : 2 * part]
        return top if level == 1 else jnp.concatenate([top, value[2 * part :]], axis=0)

    def packed(value, level):
        part = width // group_of(n_dev, level)[0]
        high, low = halves_of(value[:part])
        pieces = [high, low] if level == 1 else [high, low, value[part:]]
        return jnp.concatenate(pieces, axis=0).astype(bf16)

    def first_take(level):
        size, count = group_of(n_dev, level)
        lev = level - 1
        recv, send = getattr(r, f"recv{level}"), getattr(r, f"send{level}")
        drain(recv.at[pl.ds(1, size - 1)], r.p1_recv.at[lev])
        near = send[pos % size].astype(f32)
        far = None
        for k in range(1, size):
            value = recv[k].astype(f32)
            if count > 1 or k < size // 2:
                near = near + value
            else:
                far = value if far is None else far + value
        near = joined(near, level)
        if count == 1:
            sums[level] = (near, joined(far, level))
            return
        sums[level] = (near, None)
        hop = getattr(r, f"hop{level}")
        hop[0] = packed(near, level)
        for j in range(1, count):
            remote(hop.at[0], hop.at[j], r.p2_send.at[lev], r.p2_recv.at[lev], flip(j * OCTET))

    def second_take(level):
        size, count = group_of(n_dev, level)
        if count == 1:
            return
        hop = getattr(r, f"hop{level}")
        drain(hop.at[pl.ds(1, count - 1)], r.p2_recv.at[level - 1])
        near, far = sums[level][0], None
        for j in range(1, count):
            value = joined(hop[j].astype(f32), level)
            if j < count // 2:
                near = near + value
            else:
                far = value if far is None else far + value
        sums[level] = (near, far)

    def solve(level):
        size, count = group_of(n_dev, level)
        lev = level - 1
        near, far = sums[level]
        cols = near.shape[0]
        both = jnp.concatenate([near, far], axis=1)
        high, low = halves_of(both)
        moved = dot(jnp.concatenate([high, low], axis=0).astype(bf16), r.chosen[lev])
        kids = 1 if count > 1 else 2
        cap_high = r.caps[0, lev, pl.ds(0, kids * rank)]
        cap_low = r.caps[1, lev, pl.ds(0, kids * rank)]
        result = dot_nt(moved.astype(bf16), cap_high)
        result = result[:cols] + result[cols:] + dot_nt(moved[:cols].astype(bf16), cap_low)
        share, out = getattr(r, f"share{level}"), getattr(r, f"out{level}")
        for kid in range(kids):
            out[kid] = packed(result[:, kid * rank : (kid + 1) * rank], level)
        mine = pos % size
        for k in range(1, size):
            kid = 1 if count == 1 and k >= size // 2 else 0
            remote(
                out.at[kid], share.at[mine], r.p3_send.at[lev], r.p3_recv.at[lev], flip(k)
            )
        share[mine] = out[0]

    def gathered(level):
        size, _ = group_of(n_dev, level)
        share = getattr(r, f"share{level}")
        drain(share.at[pl.ds(0, size - 1)], r.p3_recv.at[level - 1])
        part, cut = width // size, rank // size
        top = share[:, pl.ds(0, 2 * part)].astype(f32)
        top = (top[:, :part] + top[:, part:]).reshape(width, rank)
        return [top] + [
            share[:, pl.ds(2 * part + k * cut, cut)].reshape(rank, rank) for k in range(level - 1)
        ]

    def prepare(lev):
        for copy in cap_loads[lev]:
            copy.wait()
        high, low = split(r.cap[lev])
        r.caps[0, lev] = high
        r.caps[1, lev] = low
        order = lax.broadcasted_iota(jnp.int32, (2 * rank, 2 * rank), 0)
        pivots = r.piv_ref[pl.ds(heaps[lev], 1), :]
        at = pivots + rank * (1 - odds[lev])
        at = jnp.where(at >= 2 * rank, at - 2 * rank, at)
        r.chosen[lev] = (order == at).astype(f32).astype(bf16)

    def widened(value, own_squares_at, ones_at):
        value_f = value.astype(f32)
        high, low = split(value_f * value_f)
        squares = dot(
            jnp.concatenate([high, low], axis=1), jnp.ones((2 * feat, feat), bf16)
        )
        one = squares.astype(bf16).astype(f32)
        two = (squares - one).astype(bf16).astype(f32)
        three = squares - one - two
        lane = lax.broadcasted_iota(jnp.int32, squares.shape, 1)
        extra = jnp.where((lane >= ones_at) & (lane < ones_at + 3), 1.0, 0.0)
        for i, piece in enumerate((one, two, three)):
            extra = jnp.where(lane == own_squares_at + i, -piece, extra)
        return extra.astype(bf16)

    def widen_train(which):
        value = r.train[which]
        r.train_w[which, :, pl.ds(0, feat)] = value + value
        r.train_w[which, :, pl.ds(feat, feat)] = widened(value, 3, 0)

    def widen_tests():
        def step(i, carry):
            part = pl.ds(pl.multiple_of(i * wide_rows, wide_rows), wide_rows)
            for h in range(2):
                value = r.gath[h, part]
                r.test_w[h, part, pl.ds(0, feat)] = value
                r.test_w[h, part, pl.ds(feat, feat)] = widened(value, 0, 3)
            return carry

        wide_rows = min(256, pairs * half)
        lax.fori_loop(0, pairs * half // wide_rows, step, 0)

    rate = spread_coef / feat * math.log2(math.e)
    chunk = min(128, pairs * half)

    def fill(which, h):
        def step(i, carry):
            part = pl.ds(pl.multiple_of(i * chunk, chunk), chunk)
            negative = dot_nt(r.test_w[h, part], r.train_w[which])
            r.kmat[h, part, pl.ds(which * points, points)] = jnp.exp2(rate * negative).astype(bf16)
            return carry

        lax.fori_loop(0, pairs * half // chunk, step, 0)

    train_load.wait()
    remote(r.train.at[0], r.train.at[1], r.tr_send, r.tr_recv, flip(1))
    tgt_load.wait()
    high, low = split(r.tgt[...])
    r.stack[pl.ds(0, width)] = high
    r.stack[pl.ds(width, width)] = low
    gram(1)
    widen_train(0)
    for level in range(2, LEVELS + 1):
        turn(level - 2)
        gram(level)
    for lev in range(LEVELS):
        prepare(lev)
    drain(r.gath.at[:, pl.ds(0, (pairs - 1) * half)], r.ag_recv)
    widen_tests()
    first_take(1)
    first_take(2)
    fill(0, 0)
    first_take(3)
    if group_of(n_dev, 3)[1] == 1:
        solve(3)
    second_take(1)
    solve(1)
    second_take(2)
    solve(2)
    if group_of(n_dev, 3)[1] > 1:
        second_take(3)
        solve(3)
    first_take(4)
    second_take(4)
    solve(4)
    drain(r.train.at[0], r.tr_recv)
    widen_train(1)
    fill(0, 1)
    fill(1, 0)
    fill(1, 1)
    turn(LEVELS - 1)
    zero = jnp.zeros((width, points), bf16)
    for which in range(2):
        r.wts[which, 0, pl.ds(width, width)] = zero
        r.wts[which, 1, pl.ds(0, width)] = zero

    pairs_ab = {}
    for level in range(2, LEVELS + 1):
        blocks = gathered(level)
        value = jnp.concatenate([blocks[0], blocks[1].astype(f32)], axis=0)
        for k in range(2, level):
            ab_high, ab_low = pairs_ab[k]
            value = value - dot(ab_high, blocks[k]) - dot(ab_low, blocks[k])
        pairs_ab[level] = split(value)
        r.ab[:, pl.ds((level - 2) * rank, rank)] = value
    b_high, b_low = split(r.ab[pl.ds(width, rank)])
    first = gathered(1)[0]
    s_high, s_low = split(first)
    later = r.ab[pl.ds(0, width)] - (dot(s_high, b_high) + dot(s_low, b_high) + dot(s_high, b_low))
    shares = jnp.concatenate([first, later], axis=1)
    share_high, share_low = split(shares)
    left_high = r.stack[pl.ds(2 * width, LEVELS * rank)]
    current = r.tgt[...] - (
        dot(share_high, left_high) + dot(share_low, left_high) + dot(share_high, r.ltl[...])
    )
    r.cur[...] = current
    weights = current.astype(bf16)
    r.wts[0, 0, pl.ds(0, width)] = weights
    r.wts[0, 1, pl.ds(width, width)] = weights
    r.wt[0] = weights
    remote(r.wt.at[0], r.wt.at[1], r.wt_send, r.wt_recv, flip(1))
    cur_copy = pltpu.make_async_copy(r.cur, r.cur_out, r.out_sem)
    cur_copy.start()

    big = min(256, pairs * half)

    def weigh(which):
        def step(i, carry):
            part = pl.ds(pl.multiple_of(i * big, big), big)
            there = pl.ds(which * points, points)
            value = dot_nt(r.kmat[0, part, there], r.wts[which, 0]) + dot_nt(
                r.kmat[1, part, there], r.wts[which, 1]
            )
            if which == 0:
                r.terms[part] = value
            else:
                r.term_b[part] = (r.terms[part] + value).astype(bf16)
            return carry

        lax.fori_loop(0, pairs * half // big, step, 0)

    weigh(0)
    drain(r.wt.at[1], r.wt_recv)
    weights = r.wt[1]
    r.wts[1, 0, pl.ds(0, width)] = weights
    r.wts[1, 1, pl.ds(width, width)] = weights
    weigh(1)

    def scatter(k, carry):
        to = (slot + k) % pairs
        remote(
            r.term_b.at[pl.ds(pl.multiple_of(to * half, half), half)],
            r.term_in.at[pl.ds(pl.multiple_of((k - 1) * half, half), half)],
            r.rs_send, r.rs_recv, coords(2 * to + parity),
        )
        return carry

    lax.fori_loop(1, pairs, scatter, 0)
    drain(r.gath.at[:, pl.ds(0, (pairs - 1) * half)], r.ag_send)
    drain(r.train.at[0], r.tr_send)
    drain(r.wt.at[0], r.wt_send)
    for level in range(1, LEVELS + 1):
        size, count = group_of(n_dev, level)
        lev = level - 1
        drain(getattr(r, f"recv{level}").at[pl.ds(1, size - 1)], r.p1_send.at[lev])
        if count > 1:
            drain(getattr(r, f"hop{level}").at[pl.ds(1, count - 1)], r.p2_send.at[lev])
        drain(getattr(r, f"share{level}").at[pl.ds(0, size - 1)], r.p3_send.at[lev])
    cur_copy.wait()
    total = r.term_b[own_rows].astype(f32)
    drain(r.term_in, r.rs_recv)
    total = total + jnp.sum(r.term_in[...].astype(f32).reshape(pairs - 1, half, 2 * width), axis=0)
    r.pred_out[pl.ds(0, half)] = total[:, :width]
    r.pred_out[pl.ds(half, half)] = total[:, width:]
    drain(r.term_in, r.rs_send)


def body(n_dev, narrow, targets, train, test, left, right, cap, pivots):
    points, width = targets.shape
    rank = left.shape[2]
    feat = train.shape[1]
    rows = test.shape[0]
    half = rows // 2
    pairs = n_dev // 2
    vmem = pltpu.VMEM
    dma = pltpu.SemaphoreType.DMA
    hbm_spec = pl.BlockSpec(memory_space=pl.ANY)
    vmem_spec = pl.BlockSpec(memory_space=pltpu.VMEM)
    scratch = {
        "tgt": vmem((width, points), f32),
        "train": vmem((2, points, feat), bf16),
        "gath": vmem((2, pairs * half, feat), bf16),
        "left": vmem((LEVELS, points, rank), f32),
        "right": vmem((LEVELS, points, rank), f32),
        "cap": vmem((LEVELS, 2 * rank, 2 * rank), f32),
        "caps": vmem((2, LEVELS, 2 * rank, 2 * rank), bf16),
        "chosen": vmem((LEVELS, 2 * rank, 2 * rank), bf16),
        "stack": vmem((2 * width + LEVELS * rank, points), bf16),
        "ltl": vmem((LEVELS * rank, points), bf16),
        "train_w": vmem((2, points, 2 * feat), bf16),
        "test_w": vmem((2, pairs * half, 2 * feat), bf16),
        "kmat": vmem((2, pairs * half, 2 * points), bf16),
        "ab": vmem((width + rank, (LEVELS - 1) * rank), f32),
        "cur": vmem((width, points), f32),
        "wt": vmem((2, width, points), bf16),
        "wts": vmem((2, 2, 2 * width, points), bf16),
        "terms": vmem((pairs * half, 2 * width), f32),
        "term_b": vmem((pairs * half, 2 * width), bf16),
        "term_in": vmem(((pairs - 1) * half, 2 * width), bf16),
    }
    for level in range(1, LEVELS + 1):
        size, count = group_of(n_dev, level)
        tall = (2 * width + (level - 1) * rank) // size
        for name in ("send", "recv", "share"):
            scratch[f"{name}{level}"] = vmem((size, tall, rank), bf16)
        scratch[f"out{level}"] = vmem((2, tall, rank), bf16)
        if count > 1:
            scratch[f"hop{level}"] = vmem((count, tall, rank), bf16)
    scratch["load_sem"] = dma((4 + 2 * LEVELS,))
    scratch["cap_sem"] = dma((LEVELS, 2))
    for name in ("p1_send", "p1_recv", "p2_send", "p2_recv", "p3_send", "p3_recv"):
        scratch[name] = dma((LEVELS,))
    for name in (
        "ag_send", "ag_recv", "tr_send", "tr_recv", "wt_send", "wt_recv", "rs_send", "rs_recv",
        "out_sem",
    ):
        scratch[name] = dma
    names = ["tgt_h", "train_h", "test_h", "left_h", "right_h", "cap_h", "piv_ref"]
    names += ["cur_out", "pred_out"] + list(scratch)
    current, predictions = pl.pallas_call(
        functools.partial(kernel, n_dev, narrow, names),
        out_shape=(
            jax.ShapeDtypeStruct((width, points), f32),
            jax.ShapeDtypeStruct((rows, width), f32),
        ),
        in_specs=[hbm_spec] * 6 + [vmem_spec],
        out_specs=(hbm_spec, vmem_spec),
        scratch_shapes=list(scratch.values()),
        compiler_params=pltpu.CompilerParams(
            collective_id=0, has_side_effects=True, vmem_limit_bytes=60 * 1024 * 1024
        ),
    )(targets.T, train, test, left, right, cap, pivots)
    return current.T, predictions


def solution(mesh):
    both = ("wide", "narrow")
    placed = (
        P(both, None), P(both, None), P(both, None),
        P(both, None, None), P(both, None, None), P(), P(),
    )
    sizes = dict(mesh.shape)
    return jax.shard_map(
        functools.partial(body, sizes["wide"] * sizes["narrow"], sizes["narrow"]),
        mesh=mesh,
        in_specs=placed,
        out_specs=(P(both, None), P(both, None)),
        check_vma=False,
    )
```

time: 43.8 us -> 32.3 us (0.74)
  Pallas kernels: 37.6 us -> 28.3 us
  local copies, waits for them, and re-layouts: 5.19 us -> 2.99 us
    pallas_call x1, Pallas kernels: 37.6 us -> 28.3 us  [body(): pl.pallas_call(functools.partial(kernel, n_dev, narrow, names), out_shape...]
    pallas_call x1 -> x0, local copies, waits for them, and re-layouts: 1.93 us -> none  [body(): pl.pallas_call(functools.partial(kernel, n_dev, narrow), out_shape=(jax.S...]
where the time goes in v1:
time: 32.3 us; the launch traced here: 31.9 us
  Pallas kernels  28.3 us (88%)
  local copies, waits for them, and re-layouts  2.99 us (9%)
  between operations  0.64 us (2%)
    pallas_call x1, Pallas kernels, body(): pl.pallas_call(functools.partial(kernel, n_dev, narrow, names), out_shape...  28.3 us
    unnamed x2, local copies, waits for them, and re-layouts  2.99 us

profile of v1, /device:TPU:0, one launch (start us, length us, event | category | flops | bytes accessed | tf_op | source)
XLA Modules:
  0.0 31.9 jit_solution(4319629453162828178)
XLA Ops:
  0.6 28.3 %shard_map.86 = (f32[64,1024]{1,0:T(8,128)}, f32[32,64]{1,0:T(8,128)}) custom-call(f32[64,1024]{1,0:T(8,128)} %bitcast.2, bf16[1024,128]{1,0:T(8,128)(2,1)} %refs_1_.1, bf16[32,128]{1,0:T(8,128)(2,1)} %refs_2_.1, f32[1024,4,128]{2,1,0:T(4,128)} %refs_3_.1, f32[1024,4,128]{2,1,0:T(4,128)} %refs_4_.1, f32[15,256,256]{2,1,0:T(8,128)} %refs_5_.1, s32[15,256]{1,0:T(8,128)} %refs_6_.1), custom_call_target="tpu_custom_call" | custom-call | tf_op jit(solution)/shard_map/pallas_call | solution.py:490
  28.9 1.7 %copy.11 = f32[1024,64]{0,1:T(8,128)} copy(f32[1024,64]{0,1:T(8,128)} %bitcast.3) | data formatting | bytes 524288
  30.6 1.3 %copy.12 = f32[32,64]{1,0:T(8,128)} copy(f32[32,64]{1,0:T(8,128)} %get-tuple-element.9) | data formatting | bytes 16384

commit v2 on v1

--- a/solution.py
+++ b/solution.py
@@ -51,7 +51,11 @@
     pairs = n_dev // 2
     parity = pos % 2
     slot = pos // 2
-    own_rows = pl.ds(pl.multiple_of(slot * half, half), half)
+    octets = n_dev // OCTET
+    seat = slot % (OCTET // 2)
+    own_block = seat * octets + slot // (OCTET // 2)
+    own_rows = pl.ds(pl.multiple_of(own_block * half, half), half)
+    seat_rows = pl.ds(pl.multiple_of(seat * octets * half, octets * half), octets * half)
 
     def coords(dev):
         return (dev // narrow, dev % narrow)
@@ -82,6 +86,7 @@
         for h in range(2)
     ]
     tgt_load = load(r.tgt_h, r.tgt, r.load_sem.at[2])
+    piv_load = load(r.piv_h, r.piv, r.piv_sem)
     right_loads, left_loads = [], []
     train_load = None
     for lev in range(LEVELS):
@@ -110,25 +115,13 @@
 
     def greet(k, carry):
         pl.semaphore_signal(
-            barrier, inc=1, device_id=coords((pos + 2 * k) % n_dev), device_id_type=MESH
+            barrier, inc=1, device_id=coords((pos + OCTET * k) % n_dev), device_id_type=MESH
         )
         return carry
 
-    lax.fori_loop(1, pairs, greet, 0)
-    crossing = range(1, OCTET, 2)
-    for k in crossing:
+    lax.fori_loop(1, octets, greet, 0)
+    for k in range(1, OCTET):
         pl.semaphore_signal(barrier, inc=1, device_id=flip(k), device_id_type=MESH)
-    pl.semaphore_wait(barrier, pairs - 1 + len(crossing))
-
-    for copy in test_loads:
-        copy.wait()
-    own_test = r.gath.at[:, own_rows]
-
-    def spread(k, carry):
-        remote(own_test, own_test, r.ag_send, r.ag_recv, coords((pos + 2 * k) % n_dev))
-        return carry
-
-    lax.fori_loop(1, pairs, spread, 0)
 
     def first_send(level):
         size, _ = group_of(n_dev, level)
@@ -162,7 +155,6 @@
         for k in range(lev):
             piece = product[2 * width + k * rank : 2 * width + (k + 1) * rank]
             send[:, pl.ds(2 * part + k * cut, cut)] = piece.astype(bf16).reshape(size, cut, rank)
-        first_send(level)
 
     def turn(lev):
         left_loads[lev].wait()
@@ -263,7 +255,7 @@
         r.caps[0, lev] = high
         r.caps[1, lev] = low
         order = lax.broadcasted_iota(jnp.int32, (2 * rank, 2 * rank), 0)
-        pivots = r.piv_ref[pl.ds(heaps[lev], 1), :]
+        pivots = r.piv[pl.ds(heaps[lev], 1), :]
         at = pivots + rank * (1 - odds[lev])
         at = jnp.where(at >= 2 * rank, at - 2 * rank, at)
         r.chosen[lev] = (order == at).astype(f32).astype(bf16)
@@ -312,47 +304,66 @@
 
         lax.fori_loop(0, pairs * half // chunk, step, 0)
 
-    train_load.wait()
-    remote(r.train.at[0], r.train.at[1], r.tr_send, r.tr_recv, flip(1))
     tgt_load.wait()
     high, low = split(r.tgt[...])
     r.stack[pl.ds(0, width)] = high
     r.stack[pl.ds(width, width)] = low
     gram(1)
+    turn(0)
+    gram(2)
+    for copy in test_loads:
+        copy.wait()
+    train_load.wait()
+    pl.semaphore_wait(barrier, octets - 1 + OCTET - 1)
+    first_send(1)
+    own_test = r.gath.at[:, own_rows]
+
+    def spread(k, carry):
+        remote(own_test, own_test, r.ag_send, r.ag_recv, coords((pos + OCTET * k) % n_dev))
+        return carry
+
+    lax.fori_loop(1, octets, spread, 0)
+    first_send(2)
+    remote(r.train.at[0], r.train.at[1], r.tr_send, r.tr_recv, flip(1))
+    turn(1)
+    gram(3)
+    first_send(3)
+    turn(2)
+    gram(4)
+    first_send(4)
     widen_train(0)
-    for level in range(2, LEVELS + 1):
-        turn(level - 2)
-        gram(level)
+    piv_load.wait()
     for lev in range(LEVELS):
         prepare(lev)
-    drain(r.gath.at[:, pl.ds(0, (pairs - 1) * half)], r.ag_recv)
-    widen_tests()
     first_take(1)
     first_take(2)
-    fill(0, 0)
+    drain(r.gath.at[:, pl.ds(0, (octets - 1) * half)], r.ag_recv)
+    seat_test = r.gath.at[:, seat_rows]
+    for k in range(2, OCTET, 2):
+        remote(seat_test, seat_test, r.fw_send, r.fw_recv, flip(k))
     first_take(3)
     if group_of(n_dev, 3)[1] == 1:
         solve(3)
-    second_take(1)
-    solve(1)
-    second_take(2)
-    solve(2)
-    if group_of(n_dev, 3)[1] > 1:
-        second_take(3)
-        solve(3)
     first_take(4)
-    second_take(4)
-    solve(4)
+    if group_of(n_dev, 4)[1] == 1:
+        solve(4)
     drain(r.train.at[0], r.tr_recv)
     widen_train(1)
-    fill(0, 1)
-    fill(1, 0)
-    fill(1, 1)
     turn(LEVELS - 1)
     zero = jnp.zeros((width, points), bf16)
     for which in range(2):
         r.wts[which, 0, pl.ds(width, width)] = zero
         r.wts[which, 1, pl.ds(0, width)] = zero
+    for level in (4, 3, 2, 1):
+        if group_of(n_dev, level)[1] > 1:
+            second_take(level)
+            solve(level)
+    drain(r.gath.at[:, pl.ds(0, (OCTET // 2 - 1) * octets * half)], r.fw_recv)
+    widen_tests()
+    fill(0, 0)
+    fill(0, 1)
+    fill(1, 0)
+    fill(1, 1)
 
     pairs_ab = {}
     for level in range(2, LEVELS + 1):
@@ -407,16 +418,18 @@
     weigh(1)
 
     def scatter(k, carry):
-        to = (slot + k) % pairs
+        block = (own_block + k) % pairs
+        to = (block % octets) * (OCTET // 2) + block // octets
         remote(
-            r.term_b.at[pl.ds(pl.multiple_of(to * half, half), half)],
+            r.term_b.at[pl.ds(pl.multiple_of(block * half, half), half)],
             r.term_in.at[pl.ds(pl.multiple_of((k - 1) * half, half), half)],
             r.rs_send, r.rs_recv, coords(2 * to + parity),
         )
         return carry
 
     lax.fori_loop(1, pairs, scatter, 0)
-    drain(r.gath.at[:, pl.ds(0, (pairs - 1) * half)], r.ag_send)
+    drain(r.gath.at[:, pl.ds(0, (octets - 1) * half)], r.ag_send)
+    drain(r.gath.at[:, pl.ds(0, (OCTET // 2 - 1) * octets * half)], r.fw_send)
     drain(r.train.at[0], r.tr_send)
     drain(r.wt.at[0], r.wt_send)
     for level in range(1, LEVELS + 1):
@@ -448,6 +461,7 @@
     vmem_spec = pl.BlockSpec(memory_space=pltpu.VMEM)
     scratch = {
         "tgt": vmem((width, points), f32),
+        "piv": vmem(pivots.shape, jnp.int32),
         "train": vmem((2, points, feat), bf16),
         "gath": vmem((2, pairs * half, feat), bf16),
         "left": vmem((LEVELS, points, rank), f32),
@@ -482,10 +496,10 @@
         scratch[name] = dma((LEVELS,))
     for name in (
         "ag_send", "ag_recv", "tr_send", "tr_recv", "wt_send", "wt_recv", "rs_send", "rs_recv",
-        "out_sem",
+        "out_sem", "piv_sem", "fw_send", "fw_recv",
     ):
         scratch[name] = dma
-    names = ["tgt_h", "train_h", "test_h", "left_h", "right_h", "cap_h", "piv_ref"]
+    names = ["tgt_h", "train_h", "test_h", "left_h", "right_h", "cap_h", "piv_h"]
     names += ["cur_out", "pred_out"] + list(scratch)
     current, predictions = pl.pallas_call(
         functools.partial(kernel, n_dev, narrow, names),
@@ -493,11 +507,11 @@
             jax.ShapeDtypeStruct((width, points), f32),
             jax.ShapeDtypeStruct((rows, width), f32),
         ),
-        in_specs=[hbm_spec] * 6 + [vmem_spec],
+        in_specs=[hbm_spec] * 7,
         out_specs=(hbm_spec, vmem_spec),
         scratch_shapes=list(scratch.values()),
         compiler_params=pltpu.CompilerParams(
-            collective_id=0, has_side_effects=True, vmem_limit_bytes=60 * 1024 * 1024
+            collective_id=0, has_side_effects=True, vmem_limit_bytes=48 * 1024 * 1024
         ),
     )(targets.T, train, test, left, right, cap, pivots)
     return current.T, predictions

time: 32.3 us -> 36.1 us (1.12)
  local copies, waits for them, and re-layouts: 2.99 us -> 7.8 us
  Pallas kernels: 28.3 us -> 27.3 us
    unnamed x2 -> x14, local copies, waits for them, and re-layouts: 2.99 us -> 7.8 us
    pallas_call x1, Pallas kernels: 28.3 us -> 27.3 us  [body(): pl.pallas_call(functools.partial(kernel, n_dev, narrow, names), out_shape...]
where the time goes in v2:
time: 36.1 us; the launch traced here: 35.8 us
  Pallas kernels  27.3 us (76%)
  local copies, waits for them, and re-layouts  7.8 us (22%)
  between operations  0.65 us (2%)
    pallas_call x1, Pallas kernels, body(): pl.pallas_call(functools.partial(kernel, n_dev, narrow, names), out_shape...  27.3 us
    unnamed x14, local copies, waits for them, and re-layouts  7.8 us

profile of v2, /device:TPU:0, one launch (start us, length us, event | category | flops | bytes accessed | tf_op | source)
XLA Modules:
  0.0 35.8 jit_solution(8389446944814941218)
XLA Ops:
  0.6 0.0 copy-start
  0.6 1.6 %copy-done = f32[1024,4,128]{2,1,0:T(4,128)S(1)} copy-done((f32[1024,4,128]{2,1,0:T(4,128)S(1)}, f32[1024,4,128]{2,1,0:T(4,128)}, u32[]{:S(2)}) %copy-start) | copy-done | bytes 2097176
  2.2 0.0 copy-start.1
  2.2 1.6 %copy-done.1 = f32[1024,4,128]{2,1,0:T(4,128)S(1)} copy-done((f32[1024,4,128]{2,1,0:T(4,128)S(1)}, f32[1024,4,128]{2,1,0:T(4,128)}, u32[]{:S(2)}) %copy-start.1) | copy-done | bytes 2097176
  3.8 0.0 copy-start.2
  3.8 0.9 %copy-done.2 = f32[1024,64]{0,1:T(8,128)S(1)} copy-done((f32[1024,64]{0,1:T(8,128)S(1)}, f32[1024,64]{0,1:T(8,128)}, u32[]{:S(2)}) %copy-start.2) | copy-done | bytes 262168
  4.8 0.0 copy-start.3
  4.8 0.9 %copy-done.3 = bf16[1024,128]{1,0:T(8,128)(2,1)S(1)} copy-done((bf16[1024,128]{1,0:T(8,128)(2,1)S(1)}, bf16[1024,128]{1,0:T(8,128)(2,1)}, u32[]{:S(2)}) %copy-start.3) | copy-done | bytes 262168
  5.7 0.0 copy-start.4
  5.7 0.7 %copy-done.4 = s32[15,256]{1,0:T(8,128)S(1)} copy-done((s32[15,256]{1,0:T(8,128)S(1)}, s32[15,256]{1,0:T(8,128)}, u32[]{:S(2)}) %copy-start.4) | copy-done | bytes 15384
  6.4 0.0 copy-start.5
  6.4 0.7 %copy-done.5 = bf16[32,128]{1,0:T(8,128)(2,1)S(1)} copy-done((bf16[32,128]{1,0:T(8,128)(2,1)S(1)}, bf16[32,128]{1,0:T(8,128)(2,1)}, u32[]{:S(2)}) %copy-start.5) | copy-done | bytes 8216
  7.1 27.3 %shard_map.86 = (f32[64,1024]{1,0:T(8,128)S(1)}, f32[32,64]{1,0:T(8,128)S(1)}) custom-call(f32[64,1024]{1,0:T(8,128)S(1)} %bitcast.2, bf16[1024,128]{1,0:T(8,128)(2,1)S(1)} %copy-done.3, bf16[32,128]{1,0:T(8,128)(2,1)S(1)} %copy-done.5, f32[1024,4,128]{2,1,0:T(4,128)S(1)} %copy-done, f32[1024,4,128]{2,1,0:T(4,128)S(1)} %copy-done.1, ...), custom_call_target="tpu_custom_call" | custom-call | tf_op jit(solution)/shard_map/pallas_call | solution.py:504
  34.5 0.7 %copy.11 = f32[1024,64]{0,1:T(8,128)} copy(f32[1024,64]{0,1:T(8,128)S(1)} %bitcast.3) | data formatting | bytes 524288
  35.2 0.6 %copy.12 = f32[32,64]{1,0:T(8,128)} copy(f32[32,64]{1,0:T(8,128)S(1)} %get-tuple-element.9) | data formatting | bytes 16384
Async XLA Ops:
  0.6 1.6 %copy-start = (f32[1024,4,128]{2,1,0:T(4,128)S(1)}, f32[1024,4,128]{2,1,0:T(4,128)}, u32[]{:S(2)}) copy-start(f32[1024,4,128]{2,1,0:T(4,128)} %refs_3_.1) | copy-start | bytes 6291460
  2.2 1.6 %copy-start.1 = (f32[1024,4,128]{2,1,0:T(4,128)S(1)}, f32[1024,4,128]{2,1,0:T(4,128)}, u32[]{:S(2)}) copy-start(f32[1024,4,128]{2,1,0:T(4,128)} %refs_4_.1) | copy-start | bytes 6291460
  3.8 0.9 %copy-start.2 = (f32[1024,64]{0,1:T(8,128)S(1)}, f32[1024,64]{0,1:T(8,128)}, u32[]{:S(2)}) copy-start(f32[1024,64]{0,1:T(8,128)} %param.7) | copy-start | bytes 786436
  4.8 0.9 %copy-start.3 = (bf16[1024,128]{1,0:T(8,128)(2,1)S(1)}, bf16[1024,128]{1,0:T(8,128)(2,1)}, u32[]{:S(2)}) copy-start(bf16[1024,128]{1,0:T(8,128)(2,1)} %refs_1_.1) | copy-start | bytes 786436
  5.7 0.7 %copy-start.4 = (s32[15,256]{1,0:T(8,128)S(1)}, s32[15,256]{1,0:T(8,128)}, u32[]{:S(2)}) copy-start(s32[15,256]{1,0:T(8,128)} %refs_6_.1) | copy-start | bytes 46084
  6.4 0.7 %copy-start.5 = (bf16[32,128]{1,0:T(8,128)(2,1)S(1)}, bf16[32,128]{1,0:T(8,128)(2,1)}, u32[]{:S(2)}) copy-start(bf16[32,128]{1,0:T(8,128)(2,1)} %refs_2_.1) | copy-start | bytes 24580

commit v3 on v2

--- a/solution.py
+++ b/solution.py
@@ -507,13 +507,16 @@
             jax.ShapeDtypeStruct((width, points), f32),
             jax.ShapeDtypeStruct((rows, width), f32),
         ),
-        in_specs=[hbm_spec] * 7,
+        in_specs=[pl.BlockSpec(memory_space=pltpu.HBM)] * 7,
         out_specs=(hbm_spec, vmem_spec),
         scratch_shapes=list(scratch.values()),
         compiler_params=pltpu.CompilerParams(
             collective_id=0, has_side_effects=True, vmem_limit_bytes=48 * 1024 * 1024
         ),
-    )(targets.T, train, test, left, right, cap, pivots)
+    )(*(
+        pltpu.with_memory_space_constraint(value, pltpu.HBM)
+        for value in (targets.T, train, test, left, right, cap, pivots)
+    ))
     return current.T, predictions
 
 

time: 36.1 us -> 27.3 us (0.76)
  local copies, waits for them, and re-layouts: 7.8 us -> 1.31 us
  Pallas kernels: 27.3 us -> 25.2 us
    unnamed x14 -> x2, local copies, waits for them, and re-layouts: 7.8 us -> 1.31 us
    pallas_call x1, Pallas kernels: 27.3 us -> 25.2 us  [body(): pl.pallas_call(functools.partial(kernel, n_dev, narrow, names), out_shape...]
where the time goes in v3:
time: 27.3 us; the launch traced here: 27.1 us
  Pallas kernels  25.2 us (92%)
  local copies, waits for them, and re-layouts  1.31 us (5%)
  between operations  0.64 us (2%)
    pallas_call x1, Pallas kernels, body(): pl.pallas_call(functools.partial(kernel, n_dev, narrow, names), out_shape...  25.2 us
    unnamed x2, local copies, waits for them, and re-layouts  1.31 us

profile of v3, /device:TPU:0, one launch (start us, length us, event | category | flops | bytes accessed | tf_op | source)
XLA Modules:
  0.0 27.1 jit_solution(3738669264572754069)
XLA Ops:
  0.6 25.2 %shard_map.86 = (f32[64,1024]{1,0:T(8,128)S(1)}, f32[32,64]{1,0:T(8,128)S(1)}) custom-call(f32[64,1024]{1,0:T(8,128)} %bitcast.3, bf16[1024,128]{1,0:T(8,128)(2,1)} %refs_1_.1, bf16[32,128]{1,0:T(8,128)(2,1)} %refs_2_.1, f32[1024,4,128]{2,1,0:T(4,128)} %refs_3_.1, f32[1024,4,128]{2,1,0:T(4,128)} %refs_4_.1, f32[15,256,256]{2,1,0:T(8,128)} %refs_5_.1, ...), custom_call_target="tpu_custom_call" | custom-call | tf_op jit(solution)/shard_map/pallas_call | solution.py:504
  25.8 0.7 %copy.11 = f32[1024,64]{0,1:T(8,128)} copy(f32[1024,64]{0,1:T(8,128)S(1)} %bitcast.2) | data formatting | bytes 524288
  26.5 0.6 %copy.12 = f32[32,64]{1,0:T(8,128)} copy(f32[32,64]{1,0:T(8,128)S(1)} %get-tuple-element.9) | data formatting | bytes 16384

commit v4 on v3

--- a/solution.py
+++ b/solution.py
@@ -285,24 +285,27 @@
             part = pl.ds(pl.multiple_of(i * wide_rows, wide_rows), wide_rows)
             for h in range(2):
                 value = r.gath[h, part]
-                r.test_w[h, part, pl.ds(0, feat)] = value
-                r.test_w[h, part, pl.ds(feat, feat)] = widened(value, 0, 3)
+                there = pl.ds(
+                    pl.multiple_of(h * pairs * half + i * wide_rows, wide_rows), wide_rows
+                )
+                r.test_w[there, pl.ds(0, feat)] = value
+                r.test_w[there, pl.ds(feat, feat)] = widened(value, 0, 3)
             return carry
 
         wide_rows = min(256, pairs * half)
         lax.fori_loop(0, pairs * half // wide_rows, step, 0)
 
     rate = spread_coef / feat * math.log2(math.e)
-    chunk = min(128, pairs * half)
-
-    def fill(which, h):
+    chunk = min(512, pairs * rows)
+
+    def fill(which):
         def step(i, carry):
             part = pl.ds(pl.multiple_of(i * chunk, chunk), chunk)
-            negative = dot_nt(r.test_w[h, part], r.train_w[which])
-            r.kmat[h, part, pl.ds(which * points, points)] = jnp.exp2(rate * negative).astype(bf16)
+            negative = dot_nt(r.test_w[part], r.train_w[which])
+            r.kmat[part, pl.ds(which * points, points)] = jnp.exp2(rate * negative).astype(bf16)
             return carry
 
-        lax.fori_loop(0, pairs * half // chunk, step, 0)
+        lax.fori_loop(0, pairs * rows // chunk, step, 0)
 
     tgt_load.wait()
     high, low = split(r.tgt[...])
@@ -350,20 +353,14 @@
     drain(r.train.at[0], r.tr_recv)
     widen_train(1)
     turn(LEVELS - 1)
-    zero = jnp.zeros((width, points), bf16)
-    for which in range(2):
-        r.wts[which, 0, pl.ds(width, width)] = zero
-        r.wts[which, 1, pl.ds(0, width)] = zero
     for level in (4, 3, 2, 1):
         if group_of(n_dev, level)[1] > 1:
             second_take(level)
             solve(level)
     drain(r.gath.at[:, pl.ds(0, (OCTET // 2 - 1) * octets * half)], r.fw_recv)
     widen_tests()
-    fill(0, 0)
-    fill(0, 1)
-    fill(1, 0)
-    fill(1, 1)
+    fill(0)
+    fill(1)
 
     pairs_ab = {}
     for level in range(2, LEVELS + 1):
@@ -381,13 +378,10 @@
     shares = jnp.concatenate([first, later], axis=1)
     share_high, share_low = split(shares)
     left_high = r.stack[pl.ds(2 * width, LEVELS * rank)]
-    current = r.tgt[...] - (
-        dot(share_high, left_high) + dot(share_low, left_high) + dot(share_high, r.ltl[...])
-    )
+    product = dot(jnp.concatenate([share_high, share_low], axis=0), left_high)
+    current = r.tgt[...] - (product[:width] + product[width:] + dot(share_high, r.ltl[...]))
     r.cur[...] = current
     weights = current.astype(bf16)
-    r.wts[0, 0, pl.ds(0, width)] = weights
-    r.wts[0, 1, pl.ds(width, width)] = weights
     r.wt[0] = weights
     remote(r.wt.at[0], r.wt.at[1], r.wt_send, r.wt_recv, flip(1))
     cur_copy = pltpu.make_async_copy(r.cur, r.cur_out, r.out_sem)
@@ -396,12 +390,17 @@
     big = min(256, pairs * half)
 
     def weigh(which):
+        twice = jnp.concatenate([r.wt[which], r.wt[which]], axis=0)
+        first_half = lax.broadcasted_iota(jnp.int32, (big, 2 * width), 1) < width
+
         def step(i, carry):
             part = pl.ds(pl.multiple_of(i * big, big), big)
+            other = pl.ds(pl.multiple_of(pairs * half + i * big, big), big)
             there = pl.ds(which * points, points)
-            value = dot_nt(r.kmat[0, part, there], r.wts[which, 0]) + dot_nt(
-                r.kmat[1, part, there], r.wts[which, 1]
+            value = dot_nt(
+                jnp.concatenate([r.kmat[part, there], r.kmat[other, there]], axis=0), twice
             )
+            value = jnp.where(first_half, value[:big], value[big:])
             if which == 0:
                 r.terms[part] = value
             else:
@@ -412,9 +411,6 @@
 
     weigh(0)
     drain(r.wt.at[1], r.wt_recv)
-    weights = r.wt[1]
-    r.wts[1, 0, pl.ds(0, width)] = weights
-    r.wts[1, 1, pl.ds(width, width)] = weights
     weigh(1)
 
     def scatter(k, carry):
@@ -446,6 +442,17 @@
     r.pred_out[pl.ds(0, half)] = total[:, :width]
     r.pred_out[pl.ds(half, half)] = total[:, width:]
     drain(r.term_in, r.rs_send)
+
+
+def finish(cur_in, pred_in, cur_out, pred_out, sems):
+    copies = [
+        pltpu.make_async_copy(cur_in, cur_out, sems.at[0]),
+        pltpu.make_async_copy(pred_in, pred_out, sems.at[1]),
+    ]
+    for copy in copies:
+        copy.start()
+    for copy in copies:
+        copy.wait()
 
 
 def body(n_dev, narrow, targets, train, test, left, right, cap, pivots):
@@ -472,12 +479,11 @@
         "stack": vmem((2 * width + LEVELS * rank, points), bf16),
         "ltl": vmem((LEVELS * rank, points), bf16),
         "train_w": vmem((2, points, 2 * feat), bf16),
-        "test_w": vmem((2, pairs * half, 2 * feat), bf16),
-        "kmat": vmem((2, pairs * half, 2 * points), bf16),
+        "test_w": vmem((pairs * rows, 2 * feat), bf16),
+        "kmat": vmem((pairs * rows, 2 * points), bf16),
         "ab": vmem((width + rank, (LEVELS - 1) * rank), f32),
         "cur": vmem((width, points), f32),
         "wt": vmem((2, width, points), bf16),
-        "wts": vmem((2, 2, 2 * width, points), bf16),
         "terms": vmem((pairs * half, 2 * width), f32),
         "term_b": vmem((pairs * half, 2 * width), bf16),
         "term_in": vmem(((pairs - 1) * half, 2 * width), bf16),
@@ -517,6 +523,18 @@
         pltpu.with_memory_space_constraint(value, pltpu.HBM)
         for value in (targets.T, train, test, left, right, cap, pivots)
     ))
+    current, predictions = pl.pallas_call(
+        finish,
+        out_shape=(
+            jax.ShapeDtypeStruct((width, points), f32),
+            jax.ShapeDtypeStruct((rows, width), f32),
+        ),
+        in_specs=[vmem_spec] * 2,
+        out_specs=(hbm_spec, hbm_spec),
+        scratch_shapes=[dma((2,))],
+    )(*(
+        pltpu.with_memory_space_constraint(value, pltpu.VMEM) for value in (current, predictions)
+    ))
     return current.T, predictions
 
 

time: 27.3 us -> 26.5 us (0.971)
  local copies, waits for them, and re-layouts: 1.31 us -> 0 us
  Pallas kernels: 25.2 us -> 25.7 us
    unnamed x2 -> x0, local copies, waits for them, and re-layouts: 1.31 us -> none
    pallas_call x0 -> x1, Pallas kernels: none -> 0.72 us  [body(): pl.pallas_call(finish, out_shape=(jax.ShapeDtypeStruct((width, points), f...]
where the time goes in v4:
time: 26.5 us; the launch traced here: 26.3 us
  Pallas kernels  25.7 us (97%)
  between operations  0.64 us (2%)
    pallas_call x1, Pallas kernels, body(): pl.pallas_call(functools.partial(kernel, n_dev, narrow, names), out_shape...  24.9 us
    pallas_call x1, Pallas kernels, body(): pl.pallas_call(finish, out_shape=(jax.ShapeDtypeStruct((width, points), f...  0.72 us

profile of v4, /device:TPU:0, one launch (start us, length us, event | category | flops | bytes accessed | tf_op | source)
XLA Modules:
  0.0 26.3 jit_solution(8209712652318757199)
XLA Ops:
  0.6 24.9 %shard_map.86 = (f32[64,1024]{1,0:T(8,128)S(1)}, f32[32,64]{1,0:T(8,128)S(1)}) custom-call(f32[64,1024]{1,0:T(8,128)} %bitcast.2, bf16[1024,128]{1,0:T(8,128)(2,1)} %refs_1_.1, bf16[32,128]{1,0:T(8,128)(2,1)} %refs_2_.1, f32[1024,4,128]{2,1,0:T(4,128)} %refs_3_.1, f32[1024,4,128]{2,1,0:T(4,128)} %refs_4_.1, f32[15,256,256]{2,1,0:T(8,128)} %refs_5_.1, ...), custom_call_target="tpu_custom_call" | custom-call | tf_op jit(solution)/shard_map/pallas_call | solution.py:510
  25.6 0.7 %shard_map.87 = (f32[64,1024]{1,0:T(8,128)}, f32[32,64]{1,0:T(8,128)}) custom-call(f32[64,1024]{1,0:T(8,128)S(1)} %get-tuple-element.6.cur_in, f32[32,64]{1,0:T(8,128)S(1)} %get-tuple-element.7.pred_in), custom_call_target="tpu_custom_call" | custom-call | tf_op jit(solution)/shard_map/pallas_call | solution.py:526

commit v5 on v4

--- a/solution.py
+++ b/solution.py
@@ -313,7 +313,6 @@
     r.stack[pl.ds(width, width)] = low
     gram(1)
     turn(0)
-    gram(2)
     for copy in test_loads:
         copy.wait()
     train_load.wait()
@@ -326,6 +325,7 @@
         return carry
 
     lax.fori_loop(1, octets, spread, 0)
+    gram(2)
     first_send(2)
     remote(r.train.at[0], r.train.at[1], r.tr_send, r.tr_recv, flip(1))
     turn(1)
@@ -362,20 +362,29 @@
     fill(0)
     fill(1)
 
-    pairs_ab = {}
-    for level in range(2, LEVELS + 1):
-        blocks = gathered(level)
-        value = jnp.concatenate([blocks[0], blocks[1].astype(f32)], axis=0)
-        for k in range(2, level):
-            ab_high, ab_low = pairs_ab[k]
-            value = value - dot(ab_high, blocks[k]) - dot(ab_low, blocks[k])
-        pairs_ab[level] = split(value)
-        r.ab[:, pl.ds((level - 2) * rank, rank)] = value
-    b_high, b_low = split(r.ab[pl.ds(width, rank)])
+    third, fourth = gathered(3), gathered(4)
+    high, low = split(third[0])
+    product = dot(jnp.concatenate([high, low, third[1], third[2]], axis=0), fourth[3])
+    r.base[:, pl.ds(0, rank)] = third[0]
+    r.base[:, pl.ds(rank, rank)] = fourth[0] - (product[:width] + product[width : 2 * width])
+    for k in range(2):
+        there = pl.ds(k * rank, rank)
+        r.mix[there, pl.ds(0, rank)] = third[1 + k]
+        at = 2 * width + k * rank
+        high, low = split(fourth[1 + k].astype(f32) - product[at : at + rank])
+        r.mix[there, pl.ds(rank, rank)] = high
+        r.mix_low[there] = low
+    second = gathered(2)
     first = gathered(1)[0]
-    s_high, s_low = split(first)
-    later = r.ab[pl.ds(0, width)] - (dot(s_high, b_high) + dot(s_low, b_high) + dot(s_high, b_low))
-    shares = jnp.concatenate([first, later], axis=1)
+    high, low = split(first)
+    product = dot(jnp.concatenate([high, low], axis=0), second[1])
+    upper = jnp.concatenate([first, second[0] - (product[:width] + product[width:])], axis=1)
+    high, low = split(upper)
+    product = dot(jnp.concatenate([high, low], axis=0), r.mix[...])
+    lower = r.base[...] - (product[:width] + product[width:])
+    shares = jnp.concatenate(
+        [upper, lower[:, :rank], lower[:, rank:] - dot(high, r.mix_low[...])], axis=1
+    )
     share_high, share_low = split(shares)
     left_high = r.stack[pl.ds(2 * width, LEVELS * rank)]
     product = dot(jnp.concatenate([share_high, share_low], axis=0), left_high)
@@ -397,10 +406,9 @@
             part = pl.ds(pl.multiple_of(i * big, big), big)
             other = pl.ds(pl.multiple_of(pairs * half + i * big, big), big)
             there = pl.ds(which * points, points)
-            value = dot_nt(
-                jnp.concatenate([r.kmat[part, there], r.kmat[other, there]], axis=0), twice
+            value = jnp.where(
+                first_half, dot_nt(r.kmat[part, there], twice), dot_nt(r.kmat[other, there], twice)
             )
-            value = jnp.where(first_half, value[:big], value[big:])
             if which == 0:
                 r.terms[part] = value
             else:
@@ -413,17 +421,32 @@
     drain(r.wt.at[1], r.wt_recv)
     weigh(1)
 
-    def scatter(k, carry):
-        block = (own_block + k) % pairs
-        to = (block % octets) * (OCTET // 2) + block // octets
-        remote(
-            r.term_b.at[pl.ds(pl.multiple_of(block * half, half), half)],
-            r.term_in.at[pl.ds(pl.multiple_of((k - 1) * half, half), half)],
-            r.rs_send, r.rs_recv, coords(2 * to + parity),
-        )
-        return carry
-
-    lax.fori_loop(1, pairs, scatter, 0)
+    own_copy = pltpu.make_async_copy(
+        r.term_b.at[own_rows], r.term_out.at[pl.ds((pairs - 1) * half, half)], r.own_sem
+    )
+    own_copy.start()
+    for turned in (3, 2, 1, 0):
+        base = pos
+        for bit in range(2):
+            if turned >> bit & 1:
+                base = base + (2 << bit) * (1 - 2 * ((pos // (2 << bit)) % 2))
+
+        def scatter(j, carry, base=base, turned=turned):
+            to = (base + OCTET * j) % n_dev
+            block = ((to // 2) % (OCTET // 2)) * octets + to // OCTET
+            remote(
+                r.term_b.at[pl.ds(pl.multiple_of(block * half, half), half)],
+                r.term_out.at[pl.ds(pl.multiple_of((turned * octets + j - 1) * half, half), half)],
+                r.rs_send, r.rs_recv, coords(to),
+            )
+            return carry
+
+        start = 0 if turned else 1
+        if octets <= 4:
+            for j in range(start, octets):
+                scatter(j, 0)
+        else:
+            lax.fori_loop(start, octets, scatter, 0)
     drain(r.gath.at[:, pl.ds(0, (octets - 1) * half)], r.ag_send)
     drain(r.gath.at[:, pl.ds(0, (OCTET // 2 - 1) * octets * half)], r.fw_send)
     drain(r.train.at[0], r.tr_send)
@@ -436,23 +459,24 @@
             drain(getattr(r, f"hop{level}").at[pl.ds(1, count - 1)], r.p2_send.at[lev])
         drain(getattr(r, f"share{level}").at[pl.ds(0, size - 1)], r.p3_send.at[lev])
     cur_copy.wait()
-    total = r.term_b[own_rows].astype(f32)
-    drain(r.term_in, r.rs_recv)
-    total = total + jnp.sum(r.term_in[...].astype(f32).reshape(pairs - 1, half, 2 * width), axis=0)
-    r.pred_out[pl.ds(0, half)] = total[:, :width]
-    r.pred_out[pl.ds(half, half)] = total[:, width:]
-    drain(r.term_in, r.rs_send)
-
-
-def finish(cur_in, pred_in, cur_out, pred_out, sems):
-    copies = [
-        pltpu.make_async_copy(cur_in, cur_out, sems.at[0]),
-        pltpu.make_async_copy(pred_in, pred_out, sems.at[1]),
-    ]
-    for copy in copies:
-        copy.start()
-    for copy in copies:
-        copy.wait()
+    own_copy.wait()
+    landed = r.term_out.at[pl.ds(0, (pairs - 1) * half)]
+    drain(landed, r.rs_recv)
+    drain(landed, r.rs_send)
+
+
+def finish(cur_in, terms_in, cur_out, pred_out, pred, sems):
+    cur_copy = pltpu.make_async_copy(cur_in, cur_out, sems.at[0])
+    cur_copy.start()
+    half, width = pred.shape[0] // 2, pred.shape[1]
+    terms = terms_in[...].astype(f32)
+    total = jnp.sum(terms.reshape(terms.shape[0] // half, half, 2 * width), axis=0)
+    pred[pl.ds(0, half)] = total[:, :width]
+    pred[pl.ds(half, half)] = total[:, width:]
+    pred_copy = pltpu.make_async_copy(pred, pred_out, sems.at[1])
+    pred_copy.start()
+    cur_copy.wait()
+    pred_copy.wait()
 
 
 def body(n_dev, narrow, targets, train, test, left, right, cap, pivots):
@@ -481,12 +505,13 @@
         "train_w": vmem((2, points, 2 * feat), bf16),
         "test_w": vmem((pairs * rows, 2 * feat), bf16),
         "kmat": vmem((pairs * rows, 2 * points), bf16),
-        "ab": vmem((width + rank, (LEVELS - 1) * rank), f32),
+        "base": vmem((width, 2 * rank), f32),
+        "mix": vmem((2 * rank, 2 * rank), bf16),
+        "mix_low": vmem((2 * rank, rank), bf16),
         "cur": vmem((width, points), f32),
         "wt": vmem((2, width, points), bf16),
         "terms": vmem((pairs * half, 2 * width), f32),
         "term_b": vmem((pairs * half, 2 * width), bf16),
-        "term_in": vmem(((pairs - 1) * half, 2 * width), bf16),
     }
     for level in range(1, LEVELS + 1):
         size, count = group_of(n_dev, level)
@@ -502,19 +527,19 @@
         scratch[name] = dma((LEVELS,))
     for name in (
         "ag_send", "ag_recv", "tr_send", "tr_recv", "wt_send", "wt_recv", "rs_send", "rs_recv",
-        "out_sem", "piv_sem", "fw_send", "fw_recv",
+        "out_sem", "own_sem", "piv_sem", "fw_send", "fw_recv",
     ):
         scratch[name] = dma
     names = ["tgt_h", "train_h", "test_h", "left_h", "right_h", "cap_h", "piv_h"]
-    names += ["cur_out", "pred_out"] + list(scratch)
-    current, predictions = pl.pallas_call(
+    names += ["cur_out", "term_out"] + list(scratch)
+    current, terms = pl.pallas_call(
         functools.partial(kernel, n_dev, narrow, names),
         out_shape=(
             jax.ShapeDtypeStruct((width, points), f32),
-            jax.ShapeDtypeStruct((rows, width), f32),
+            jax.ShapeDtypeStruct((pairs * half, 2 * width), bf16),
         ),
         in_specs=[pl.BlockSpec(memory_space=pltpu.HBM)] * 7,
-        out_specs=(hbm_spec, vmem_spec),
+        out_specs=(hbm_spec, hbm_spec),
         scratch_shapes=list(scratch.values()),
         compiler_params=pltpu.CompilerParams(
             collective_id=0, has_side_effects=True, vmem_limit_bytes=48 * 1024 * 1024
@@ -531,9 +556,9 @@
         ),
         in_specs=[vmem_spec] * 2,
         out_specs=(hbm_spec, hbm_spec),
-        scratch_shapes=[dma((2,))],
+        scratch_shapes=[vmem((rows, width), f32), dma((2,))],
     )(*(
-        pltpu.with_memory_space_constraint(value, pltpu.VMEM) for value in (current, predictions)
+        pltpu.with_memory_space_constraint(value, pltpu.VMEM) for value in (current, terms)
     ))
     return current.T, predictions
 

time: 26.5 us -> 25.8 us (0.974)
  Pallas kernels: 25.7 us -> 25.1 us
    pallas_call x1, Pallas kernels: 24.9 us -> 24.3 us  [body(): pl.pallas_call(functools.partial(kernel, n_dev, narrow, names), out_shape...]
where the time goes in v5:
time: 25.8 us; the launch traced here: 25.7 us
  Pallas kernels  25.1 us (97%)
  between operations  0.64 us (2%)
    pallas_call x1, Pallas kernels, body(): pl.pallas_call(functools.partial(kernel, n_dev, narrow, names), out_shape...  24.3 us
    pallas_call x1, Pallas kernels, body(): pl.pallas_call(finish, out_shape=(jax.ShapeDtypeStruct((width, points), f...  0.72 us

profile of v5, /device:TPU:0, one launch (start us, length us, event | category | flops | bytes accessed | tf_op | source)
XLA Modules:
  0.0 25.7 jit_solution(4691180795564140297)
XLA Ops:
  0.6 24.3 %shard_map.86 = (f32[64,1024]{1,0:T(8,128)S(1)}, bf16[256,128]{1,0:T(8,128)(2,1)S(1)}) custom-call(f32[64,1024]{1,0:T(8,128)} %bitcast.2, bf16[1024,128]{1,0:T(8,128)(2,1)} %refs_1_.1, bf16[32,128]{1,0:T(8,128)(2,1)} %refs_2_.1, f32[1024,4,128]{2,1,0:T(4,128)} %refs_3_.1, f32[1024,4,128]{2,1,0:T(4,128)} %refs_4_.1, f32[15,256,256]{2,1,0:T(8,128)} %refs_5_.1, ...), custom_call_target="tpu_custom_call" | custom-call | tf_op jit(solution)/shard_map/pallas_call | solution.py:535
  25.0 0.7 %shard_map.87 = (f32[64,1024]{1,0:T(8,128)}, f32[32,64]{1,0:T(8,128)}) custom-call(f32[64,1024]{1,0:T(8,128)S(1)} %get-tuple-element.6.cur_in, bf16[256,128]{1,0:T(8,128)(2,1)S(1)} %get-tuple-element.7.terms_in), custom_call_target="tpu_custom_call" | custom-call | tf_op jit(solution)/shard_map/pallas_call | solution.py:551

commit v6 on v5

--- a/solution.py
+++ b/solution.py
@@ -44,10 +44,10 @@
     r = types.SimpleNamespace(**dict(zip(names, refs)))
     pos = lax.axis_index("wide") * narrow + lax.axis_index("narrow")
     width, points = r.tgt.shape
-    rank = r.right.shape[2]
+    rank = r.right_h.shape[2]
     feat = r.train.shape[2]
-    rows = r.test_h.shape[0]
-    half = rows // 2
+    half = r.test_h.shape[1]
+    rows = 2 * half
     pairs = n_dev // 2
     parity = pos % 2
     slot = pos // 2
@@ -81,36 +81,6 @@
         copy.start()
         return copy
 
-    test_loads = [
-        load(r.test_h.at[pl.ds(h * half, half)], r.gath.at[h, own_rows], r.load_sem.at[0 + h])
-        for h in range(2)
-    ]
-    tgt_load = load(r.tgt_h, r.tgt, r.load_sem.at[2])
-    piv_load = load(r.piv_h, r.piv, r.piv_sem)
-    right_loads, left_loads = [], []
-    train_load = None
-    for lev in range(LEVELS):
-        right_loads.append(load(r.right_h.at[:, lev, :], r.right.at[lev], r.load_sem.at[4 + lev]))
-        if lev == 0:
-            train_load = load(r.train_h, r.train.at[0], r.load_sem.at[3])
-        left_loads.append(
-            load(r.left_h.at[:, lev, :], r.left.at[lev], r.load_sem.at[4 + LEVELS + lev])
-        )
-    cap_loads, odds, heaps = [], [], []
-    for level in range(1, LEVELS + 1):
-        child = pos // (n_dev >> level)
-        odd = child % 2
-        odds.append(odd)
-        heaps.append((1 << level - 1) - 1 + child // 2)
-        cap_loads.append([
-            load(
-                r.cap_h.at[heaps[-1], pl.ds(pl.multiple_of(which * rank, rank), rank)],
-                r.cap.at[level - 1, pl.ds(at * rank, rank)],
-                r.cap_sem.at[level - 1, at],
-            )
-            for at, which in enumerate((odd, 1 - odd))
-        ])
-
     barrier = pltpu.get_barrier_semaphore()
 
     def greet(k, carry):
@@ -122,6 +92,24 @@
     lax.fori_loop(1, octets, greet, 0)
     for k in range(1, OCTET):
         pl.semaphore_signal(barrier, inc=1, device_id=flip(k), device_id_type=MESH)
+
+    def side(i, count=1):
+        return pl.ds(i * points, count * points)
+
+    tgt_load = load(r.tgt_h, r.tgt, r.load_sem.at[0])
+    for i in range(2 * LEVELS):
+        source = (r.right_h, r.left_h)[i % 2].at[:, i // 2, :]
+        load(source, r.side.at[side(i)], r.side_sem.at[(i + 1) // 2])
+        if i == 0:
+            test_load = load(r.test_h, r.gath.at[:, own_rows], r.load_sem.at[1])
+            train_load = load(r.train_h, r.train.at[0], r.load_sem.at[2])
+    piv_load = load(r.piv_h, r.piv, r.load_sem.at[3])
+    odds, heaps = [], []
+    for level in range(1, LEVELS + 1):
+        child = pos // (n_dev >> level)
+        odds.append(child % 2)
+        heaps.append((1 << level - 1) - 1 + child // 2)
+        load(r.cap_h.at[heaps[-1]], r.cap.at[level - 1], r.load_sem.at[4])
 
     def first_send(level):
         size, _ = group_of(n_dev, level)
@@ -134,14 +122,15 @@
                     to = to + (1 << bit) * (1 - 2 * ((mine // (1 << bit)) % 2))
             remote(
                 getattr(r, f"send{level}").at[to], getattr(r, f"recv{level}").at[k],
-                r.p1_send.at[lev], r.p1_recv.at[lev], flip(k),
+                r.all_send, r.p1_recv.at[lev], flip(k),
             )
 
     def gram(level):
         lev = level - 1
         size, _ = group_of(n_dev, level)
-        right_loads[lev].wait()
-        high, low = split(r.right[lev])
+        if level == 1:
+            drain(r.side.at[side(0)], r.side_sem.at[0])
+        high, low = split(r.side[side(2 * lev)])
         product = dot(r.stack[pl.ds(0, 2 * width + lev * rank)], high)
         t = product[:width] + product[width : 2 * width] + dot(r.stack[pl.ds(0, width)], low)
         t_high, t_low = halves_of(t)
@@ -157,8 +146,8 @@
             send[:, pl.ds(2 * part + k * cut, cut)] = piece.astype(bf16).reshape(size, cut, rank)
 
     def turn(lev):
-        left_loads[lev].wait()
-        high, low = split(r.left[lev].T)
+        drain(r.side.at[side(2 * lev + 1, min(2, 2 * LEVELS - 1 - 2 * lev))], r.side_sem.at[lev + 1])
+        high, low = split(r.side[side(2 * lev + 1)].T)
         r.stack[pl.ds(2 * width + lev * rank, rank)] = high
         r.ltl[pl.ds(lev * rank, rank)] = low
 
@@ -196,7 +185,7 @@
         hop = getattr(r, f"hop{level}")
         hop[0] = packed(near, level)
         for j in range(1, count):
-            remote(hop.at[0], hop.at[j], r.p2_send.at[lev], r.p2_recv.at[lev], flip(j * OCTET))
+            remote(hop.at[0], hop.at[j], r.all_send, r.p2_recv.at[lev], flip(j * OCTET))
 
     def second_take(level):
         size, count = group_of(n_dev, level)
@@ -221,9 +210,10 @@
         both = jnp.concatenate([near, far], axis=1)
         high, low = halves_of(both)
         moved = dot(jnp.concatenate([high, low], axis=0).astype(bf16), r.chosen[lev])
+        odd = odds[lev]
         kids = 1 if count > 1 else 2
-        cap_high = r.caps[0, lev, pl.ds(0, kids * rank)]
-        cap_low = r.caps[1, lev, pl.ds(0, kids * rank)]
+        taken = pl.ds(pl.multiple_of(odd * rank, rank), rank) if kids == 1 else pl.ds(0, 2 * rank)
+        cap_high, cap_low = r.caps[0, lev, taken], r.caps[1, lev, taken]
         result = dot_nt(moved.astype(bf16), cap_high)
         result = result[:cols] + result[cols:] + dot_nt(moved[:cols].astype(bf16), cap_low)
         share, out = getattr(r, f"share{level}"), getattr(r, f"out{level}")
@@ -231,11 +221,11 @@
             out[kid] = packed(result[:, kid * rank : (kid + 1) * rank], level)
         mine = pos % size
         for k in range(1, size):
-            kid = 1 if count == 1 and k >= size // 2 else 0
+            kid = 0 if kids == 1 else odd if k < size // 2 else 1 - odd
             remote(
-                out.at[kid], share.at[mine], r.p3_send.at[lev], r.p3_recv.at[lev], flip(k)
+                out.at[kid], share.at[mine], r.all_send, r.p3_recv.at[lev], flip(k)
             )
-        share[mine] = out[0]
+        share[mine] = out[0 if kids == 1 else odd]
 
     def gathered(level):
         size, _ = group_of(n_dev, level)
@@ -249,8 +239,6 @@
         ]
 
     def prepare(lev):
-        for copy in cap_loads[lev]:
-            copy.wait()
         high, low = split(r.cap[lev])
         r.caps[0, lev] = high
         r.caps[1, lev] = low
@@ -313,21 +301,20 @@
     r.stack[pl.ds(width, width)] = low
     gram(1)
     turn(0)
-    for copy in test_loads:
-        copy.wait()
+    test_load.wait()
     train_load.wait()
     pl.semaphore_wait(barrier, octets - 1 + OCTET - 1)
     first_send(1)
     own_test = r.gath.at[:, own_rows]
 
     def spread(k, carry):
-        remote(own_test, own_test, r.ag_send, r.ag_recv, coords((pos + OCTET * k) % n_dev))
+        remote(own_test, own_test, r.all_send, r.ag_recv, coords((pos + OCTET * k) % n_dev))
         return carry
 
     lax.fori_loop(1, octets, spread, 0)
     gram(2)
     first_send(2)
-    remote(r.train.at[0], r.train.at[1], r.tr_send, r.tr_recv, flip(1))
+    remote(r.train.at[0], r.train.at[1], r.all_send, r.tr_recv, flip(1))
     turn(1)
     gram(3)
     first_send(3)
@@ -336,6 +323,7 @@
     first_send(4)
     widen_train(0)
     piv_load.wait()
+    drain(r.cap, r.load_sem.at[4])
     for lev in range(LEVELS):
         prepare(lev)
     first_take(1)
@@ -343,7 +331,7 @@
     drain(r.gath.at[:, pl.ds(0, (octets - 1) * half)], r.ag_recv)
     seat_test = r.gath.at[:, seat_rows]
     for k in range(2, OCTET, 2):
-        remote(seat_test, seat_test, r.fw_send, r.fw_recv, flip(k))
+        remote(seat_test, seat_test, r.all_send, r.fw_recv, flip(k))
     first_take(3)
     if group_of(n_dev, 3)[1] == 1:
         solve(3)
@@ -374,25 +362,33 @@
         high, low = split(fourth[1 + k].astype(f32) - product[at : at + rank])
         r.mix[there, pl.ds(rank, rank)] = high
         r.mix_low[there] = low
+    base_high, base_low = split(r.base[...])
+    mixed = jnp.concatenate([base_high, base_low, r.mix[...]], axis=0)
+    mixed_high = jnp.concatenate([base_high, r.mix[...]], axis=0)
+    wide = min(512, points)
+    for i in range(points // wide):
+        cut = pl.ds(i * wide, wide)
+        top = dot(mixed, r.stack[pl.ds(2 * width + 2 * rank, 2 * rank), cut])
+        bottom = dot(mixed_high, r.ltl[pl.ds(2 * rank, 2 * rank), cut])
+        r.cur0[:, cut] = r.tgt[:, cut] - (top[:width] + top[width : 2 * width] + bottom[:width])
+        rest = dot(r.mix_low[...], r.stack[pl.ds(2 * width + 3 * rank, rank), cut])
+        own = r.stack[pl.ds(2 * width, 2 * rank), cut].astype(f32)
+        own = own + r.ltl[pl.ds(0, 2 * rank), cut].astype(f32)
+        high, low = split(own - (top[2 * width :] + bottom[width:] + rest))
+        r.leff[0, :, cut] = high
+        r.leff[1, :, cut] = low
     second = gathered(2)
     first = gathered(1)[0]
     high, low = split(first)
     product = dot(jnp.concatenate([high, low], axis=0), second[1])
     upper = jnp.concatenate([first, second[0] - (product[:width] + product[width:])], axis=1)
     high, low = split(upper)
-    product = dot(jnp.concatenate([high, low], axis=0), r.mix[...])
-    lower = r.base[...] - (product[:width] + product[width:])
-    shares = jnp.concatenate(
-        [upper, lower[:, :rank], lower[:, rank:] - dot(high, r.mix_low[...])], axis=1
-    )
-    share_high, share_low = split(shares)
-    left_high = r.stack[pl.ds(2 * width, LEVELS * rank)]
-    product = dot(jnp.concatenate([share_high, share_low], axis=0), left_high)
-    current = r.tgt[...] - (product[:width] + product[width:] + dot(share_high, r.ltl[...]))
+    product = dot(jnp.concatenate([high, low], axis=0), r.leff[0])
+    current = r.cur0[...] - (product[:width] + product[width:] + dot(high, r.leff[1]))
     r.cur[...] = current
     weights = current.astype(bf16)
     r.wt[0] = weights
-    remote(r.wt.at[0], r.wt.at[1], r.wt_send, r.wt_recv, flip(1))
+    remote(r.wt.at[0], r.wt.at[1], r.all_send, r.wt_recv, flip(1))
     cur_copy = pltpu.make_async_copy(r.cur, r.cur_out, r.out_sem)
     cur_copy.start()
 
@@ -437,7 +433,7 @@
             remote(
                 r.term_b.at[pl.ds(pl.multiple_of(block * half, half), half)],
                 r.term_out.at[pl.ds(pl.multiple_of((turned * octets + j - 1) * half, half), half)],
-                r.rs_send, r.rs_recv, coords(to),
+                r.all_send, r.rs_recv, coords(to),
             )
             return carry
 
@@ -447,22 +443,17 @@
                 scatter(j, 0)
         else:
             lax.fori_loop(start, octets, scatter, 0)
-    drain(r.gath.at[:, pl.ds(0, (octets - 1) * half)], r.ag_send)
-    drain(r.gath.at[:, pl.ds(0, (OCTET // 2 - 1) * octets * half)], r.fw_send)
-    drain(r.train.at[0], r.tr_send)
-    drain(r.wt.at[0], r.wt_send)
-    for level in range(1, LEVELS + 1):
-        size, count = group_of(n_dev, level)
-        lev = level - 1
-        drain(getattr(r, f"recv{level}").at[pl.ds(1, size - 1)], r.p1_send.at[lev])
-        if count > 1:
-            drain(getattr(r, f"hop{level}").at[pl.ds(1, count - 1)], r.p2_send.at[lev])
-        drain(getattr(r, f"share{level}").at[pl.ds(0, size - 1)], r.p3_send.at[lev])
     cur_copy.wait()
     own_copy.wait()
     landed = r.term_out.at[pl.ds(0, (pairs - 1) * half)]
     drain(landed, r.rs_recv)
-    drain(landed, r.rs_send)
+    sent = 2 * points * feat + 2 * width * points
+    sent += 2 * 2 * half * feat * (octets - 1 + (OCTET // 2 - 1) * octets) + 2 * (pairs - 1) * half * 2 * width
+    for level in range(1, LEVELS + 1):
+        size, count = group_of(n_dev, level)
+        piece = 2 * getattr(r, f"send{level}").shape[1] * rank
+        sent += piece * (2 * (size - 1) + count - 1)
+    drain(r.side.at[pl.ds(0, sent // (4 * rank))], r.all_send)
 
 
 def finish(cur_in, terms_in, cur_out, pred_out, pred, sems):
@@ -495,8 +486,9 @@
         "piv": vmem(pivots.shape, jnp.int32),
         "train": vmem((2, points, feat), bf16),
         "gath": vmem((2, pairs * half, feat), bf16),
-        "left": vmem((LEVELS, points, rank), f32),
-        "right": vmem((LEVELS, points, rank), f32),
+        "side": vmem((2 * LEVELS * points, rank), f32),
+        "cur0": vmem((width, points), f32),
+        "leff": vmem((2, 2 * rank, points), bf16),
         "cap": vmem((LEVELS, 2 * rank, 2 * rank), f32),
         "caps": vmem((2, LEVELS, 2 * rank, 2 * rank), bf16),
         "chosen": vmem((LEVELS, 2 * rank, 2 * rank), bf16),
@@ -521,13 +513,13 @@
         scratch[f"out{level}"] = vmem((2, tall, rank), bf16)
         if count > 1:
             scratch[f"hop{level}"] = vmem((count, tall, rank), bf16)
-    scratch["load_sem"] = dma((4 + 2 * LEVELS,))
-    scratch["cap_sem"] = dma((LEVELS, 2))
-    for name in ("p1_send", "p1_recv", "p2_send", "p2_recv", "p3_send", "p3_recv"):
-        scratch[name] = dma((LEVELS,))
+    scratch["load_sem"] = dma((5,))
+    scratch["side_sem"] = dma((LEVELS + 1,))
+    scratch["p1_recv"] = dma((LEVELS,))
+    scratch["p2_recv"] = dma((sum(group_of(n_dev, i + 1)[1] > 1 for i in range(LEVELS)),))
+    scratch["p3_recv"] = dma((LEVELS,))
     for name in (
-        "ag_send", "ag_recv", "tr_send", "tr_recv", "wt_send", "wt_recv", "rs_send", "rs_recv",
-        "out_sem", "own_sem", "piv_sem", "fw_send", "fw_recv",
+        "all_send", "ag_recv", "fw_recv", "tr_recv", "wt_recv", "rs_recv", "out_sem", "own_sem",
     ):
         scratch[name] = dma
     names = ["tgt_h", "train_h", "test_h", "left_h", "right_h", "cap_h", "piv_h"]
@@ -546,7 +538,9 @@
         ),
     )(*(
         pltpu.with_memory_space_constraint(value, pltpu.HBM)
-        for value in (targets.T, train, test, left, right, cap, pivots)
+        for value in (
+            targets.T, train, test.reshape(2, half, feat), left, right, cap, pivots
+        )
     ))
     current, predictions = pl.pallas_call(
         finish,

time: 25.8 us -> 25.4 us (0.984)
  Pallas kernels: 25.1 us -> 24.6 us
    pallas_call x1, Pallas kernels: 24.3 us -> 23.9 us  [body(): pl.pallas_call(functools.partial(kernel, n_dev, narrow, names), out_shape...]
where the time goes in v6:
time: 25.4 us; the launch traced here: 25.3 us
  Pallas kernels  24.6 us (97%)
  between operations  0.64 us (3%)
    pallas_call x1, Pallas kernels, body(): pl.pallas_call(functools.partial(kernel, n_dev, narrow, names), out_shape...  23.9 us
    pallas_call x1, Pallas kernels, body(): pl.pallas_call(finish, out_shape=(jax.ShapeDtypeStruct((width, points), f...  0.72 us

profile of v6, /device:TPU:0, one launch (start us, length us, event | category | flops | bytes accessed | tf_op | source)
XLA Modules:
  0.0 25.3 jit_solution(6427095288641124704)
XLA Ops:
  0.6 23.9 %shard_map.86 = (f32[64,1024]{1,0:T(8,128)S(1)}, bf16[256,128]{1,0:T(8,128)(2,1)S(1)}) custom-call(f32[64,1024]{1,0:T(8,128)} %bitcast.3, bf16[1024,128]{1,0:T(8,128)(2,1)} %refs_1_.1, bf16[2,16,128]{2,1,0:T(8,128)(2,1)} %bitcast.4, f32[1024,4,128]{2,1,0:T(4,128)} %refs_3_.1, f32[1024,4,128]{2,1,0:T(4,128)} %refs_4_.1, f32[15,256,256]{2,1,0:T(8,128)} %refs_5_.1, ...), custom_call_target="tpu_custom_call" | custom-call | tf_op jit(solution)/shard_map/pallas_call | solution.py:527
  24.6 0.7 %shard_map.87 = (f32[64,1024]{1,0:T(8,128)}, f32[32,64]{1,0:T(8,128)}) custom-call(f32[64,1024]{1,0:T(8,128)S(1)} %get-tuple-element.6.cur_in, bf16[256,128]{1,0:T(8,128)(2,1)S(1)} %get-tuple-element.7.terms_in), custom_call_target="tpu_custom_call" | custom-call | tf_op jit(solution)/shard_map/pallas_call | solution.py:545

commit v7 on v6

--- a/solution.py
+++ b/solution.py
@@ -32,6 +32,10 @@
 def halves_of(value):
     high = value.astype(bf16).astype(f32)
     return high, value - high
+
+
+def far_first(size):
+    return sorted(range(1, size), key=lambda k: -(k >> 1).bit_count())
 
 
 def group_of(n_dev, level):
@@ -89,20 +93,22 @@
         )
         return carry
 
+    def side(i, count=1):
+        return pl.ds(i * points, count * points)
+
+    def load_side(i):
+        source = (r.right_h, r.left_h)[i % 2].at[:, i // 2, :]
+        load(source, r.side.at[side(i)], r.side_sem.at[(i + 1) // 2])
+
+    tgt_load = load(r.tgt_h, r.tgt, r.load_sem.at[0])
+    load_side(0)
     lax.fori_loop(1, octets, greet, 0)
     for k in range(1, OCTET):
         pl.semaphore_signal(barrier, inc=1, device_id=flip(k), device_id_type=MESH)
-
-    def side(i, count=1):
-        return pl.ds(i * points, count * points)
-
-    tgt_load = load(r.tgt_h, r.tgt, r.load_sem.at[0])
-    for i in range(2 * LEVELS):
-        source = (r.right_h, r.left_h)[i % 2].at[:, i // 2, :]
-        load(source, r.side.at[side(i)], r.side_sem.at[(i + 1) // 2])
-        if i == 0:
-            test_load = load(r.test_h, r.gath.at[:, own_rows], r.load_sem.at[1])
-            train_load = load(r.train_h, r.train.at[0], r.load_sem.at[2])
+    test_load = load(r.test_h, r.gath.at[:, own_rows], r.load_sem.at[1])
+    train_load = load(r.train_h, r.train.at[0], r.load_sem.at[2])
+    for i in range(1, 2 * LEVELS):
+        load_side(i)
     piv_load = load(r.piv_h, r.piv, r.load_sem.at[3])
     odds, heaps = [], []
     for level in range(1, LEVELS + 1):
@@ -115,7 +121,7 @@
         size, _ = group_of(n_dev, level)
         mine = pos % size
         lev = level - 1
-        for k in range(1, size):
+        for k in far_first(size):
             to = mine
             for bit in range(k.bit_length()):
                 if k >> bit & 1:
@@ -184,7 +190,7 @@
         sums[level] = (near, None)
         hop = getattr(r, f"hop{level}")
         hop[0] = packed(near, level)
-        for j in range(1, count):
+        for j in range(count - 1, 0, -1):
             remote(hop.at[0], hop.at[j], r.all_send, r.p2_recv.at[lev], flip(j * OCTET))
 
     def second_take(level):
@@ -220,7 +226,7 @@
         for kid in range(kids):
             out[kid] = packed(result[:, kid * rank : (kid + 1) * rank], level)
         mine = pos % size
-        for k in range(1, size):
+        for k in far_first(size):
             kid = 0 if kids == 1 else odd if k < size // 2 else 1 - odd
             remote(
                 out.at[kid], share.at[mine], r.all_send, r.p3_recv.at[lev], flip(k)
@@ -300,9 +306,7 @@
     r.stack[pl.ds(0, width)] = high
     r.stack[pl.ds(width, width)] = low
     gram(1)
-    turn(0)
     test_load.wait()
-    train_load.wait()
     pl.semaphore_wait(barrier, octets - 1 + OCTET - 1)
     first_send(1)
     own_test = r.gath.at[:, own_rows]
@@ -312,8 +316,10 @@
         return carry
 
     lax.fori_loop(1, octets, spread, 0)
+    turn(0)
     gram(2)
     first_send(2)
+    train_load.wait()
     remote(r.train.at[0], r.train.at[1], r.all_send, r.tr_recv, flip(1))
     turn(1)
     gram(3)
@@ -387,35 +393,41 @@
     current = r.cur0[...] - (product[:width] + product[width:] + dot(high, r.leff[1]))
     r.cur[...] = current
     weights = current.astype(bf16)
-    r.wt[0] = weights
-    remote(r.wt.at[0], r.wt.at[1], r.all_send, r.wt_recv, flip(1))
+    for h in range(2):
+        r.wt[0, h] = weights[:, h * (points // 2) : (h + 1) * (points // 2)]
+    for h in range(2):
+        remote(r.wt.at[0, h], r.wt.at[1, h], r.all_send, r.wt_recv.at[h], flip(1))
     cur_copy = pltpu.make_async_copy(r.cur, r.cur_out, r.out_sem)
     cur_copy.start()
 
     big = min(256, pairs * half)
 
-    def weigh(which):
-        twice = jnp.concatenate([r.wt[which], r.wt[which]], axis=0)
+    def weigh(which, h):
+        twice = jnp.concatenate([r.wt[which, h], r.wt[which, h]], axis=0)
         first_half = lax.broadcasted_iota(jnp.int32, (big, 2 * width), 1) < width
 
         def step(i, carry):
             part = pl.ds(pl.multiple_of(i * big, big), big)
             other = pl.ds(pl.multiple_of(pairs * half + i * big, big), big)
-            there = pl.ds(which * points, points)
+            there = pl.ds((2 * which + h) * (points // 2), points // 2)
             value = jnp.where(
                 first_half, dot_nt(r.kmat[part, there], twice), dot_nt(r.kmat[other, there], twice)
             )
-            if which == 0:
+            if which or h:
+                value = r.terms[part] + value
+            if which and h:
+                r.term_b[part] = value.astype(bf16)
+            else:
                 r.terms[part] = value
-            else:
-                r.term_b[part] = (r.terms[part] + value).astype(bf16)
             return carry
 
         lax.fori_loop(0, pairs * half // big, step, 0)
 
-    weigh(0)
-    drain(r.wt.at[1], r.wt_recv)
-    weigh(1)
+    for which in range(2):
+        for h in range(2):
+            if which:
+                drain(r.wt.at[1, h], r.wt_recv.at[h])
+            weigh(which, h)
 
     own_copy = pltpu.make_async_copy(
         r.term_b.at[own_rows], r.term_out.at[pl.ds((pairs - 1) * half, half)], r.own_sem
@@ -457,17 +469,25 @@
 
 
 def finish(cur_in, terms_in, cur_out, pred_out, pred, sems):
-    cur_copy = pltpu.make_async_copy(cur_in, cur_out, sems.at[0])
-    cur_copy.start()
+    parts = sems.shape[0] - 1
+    tall = cur_in.shape[0] // parts
+    copies = [
+        pltpu.make_async_copy(
+            cur_in.at[pl.ds(i * tall, tall)], cur_out.at[pl.ds(i * tall, tall)], sems.at[i]
+        )
+        for i in range(parts)
+    ]
+    for copy in copies:
+        copy.start()
     half, width = pred.shape[0] // 2, pred.shape[1]
     terms = terms_in[...].astype(f32)
     total = jnp.sum(terms.reshape(terms.shape[0] // half, half, 2 * width), axis=0)
     pred[pl.ds(0, half)] = total[:, :width]
     pred[pl.ds(half, half)] = total[:, width:]
-    pred_copy = pltpu.make_async_copy(pred, pred_out, sems.at[1])
-    pred_copy.start()
-    cur_copy.wait()
-    pred_copy.wait()
+    copies.append(pltpu.make_async_copy(pred, pred_out, sems.at[parts]))
+    copies[-1].start()
+    for copy in copies:
+        copy.wait()
 
 
 def body(n_dev, narrow, targets, train, test, left, right, cap, pivots):
@@ -501,7 +521,7 @@
         "mix": vmem((2 * rank, 2 * rank), bf16),
         "mix_low": vmem((2 * rank, rank), bf16),
         "cur": vmem((width, points), f32),
-        "wt": vmem((2, width, points), bf16),
+        "wt": vmem((2, 2, width, points // 2), bf16),
         "terms": vmem((pairs * half, 2 * width), f32),
         "term_b": vmem((pairs * half, 2 * width), bf16),
     }
@@ -515,11 +535,12 @@
             scratch[f"hop{level}"] = vmem((count, tall, rank), bf16)
     scratch["load_sem"] = dma((5,))
     scratch["side_sem"] = dma((LEVELS + 1,))
+    scratch["wt_recv"] = dma((2,))
     scratch["p1_recv"] = dma((LEVELS,))
     scratch["p2_recv"] = dma((sum(group_of(n_dev, i + 1)[1] > 1 for i in range(LEVELS)),))
     scratch["p3_recv"] = dma((LEVELS,))
     for name in (
-        "all_send", "ag_recv", "fw_recv", "tr_recv", "wt_recv", "rs_recv", "out_sem", "own_sem",
+        "all_send", "ag_recv", "fw_recv", "tr_recv", "rs_recv", "out_sem", "own_sem",
     ):
         scratch[name] = dma
     names = ["tgt_h", "train_h", "test_h", "left_h", "right_h", "cap_h", "piv_h"]
@@ -550,7 +571,7 @@
         ),
         in_specs=[vmem_spec] * 2,
         out_specs=(hbm_spec, hbm_spec),
-        scratch_shapes=[vmem((rows, width), f32), dma((2,))],
+        scratch_shapes=[vmem((rows, width), f32), dma((5,))],
     )(*(
         pltpu.with_memory_space_constraint(value, pltpu.VMEM) for value in (current, terms)
     ))

time: 25.4 us -> 24.9 us (0.980)
  Pallas kernels: 24.6 us -> 24.2 us
    pallas_call x1, Pallas kernels: 23.9 us -> 23.4 us  [body(): pl.pallas_call(functools.partial(kernel, n_dev, narrow, names), out_shape...]
where the time goes in v7:
time: 24.9 us; the launch traced here: 24.8 us
  Pallas kernels  24.2 us (97%)
  between operations  0.64 us (3%)
    pallas_call x1, Pallas kernels, body(): pl.pallas_call(functools.partial(kernel, n_dev, narrow, names), out_shape...  23.4 us
    pallas_call x1, Pallas kernels, body(): pl.pallas_call(finish, out_shape=(jax.ShapeDtypeStruct((width, points), f...  0.74 us

profile of v7, /device:TPU:0, one launch (start us, length us, event | category | flops | bytes accessed | tf_op | source)
XLA Modules:
  0.0 24.8 jit_solution(11183955481236968812)
XLA Ops:
  0.6 23.4 %shard_map.86 = (f32[64,1024]{1,0:T(8,128)S(1)}, bf16[256,128]{1,0:T(8,128)(2,1)S(1)}) custom-call(f32[64,1024]{1,0:T(8,128)} %bitcast.3, bf16[1024,128]{1,0:T(8,128)(2,1)} %refs_1_.1, bf16[2,16,128]{2,1,0:T(8,128)(2,1)} %bitcast.4, f32[1024,4,128]{2,1,0:T(4,128)} %refs_3_.1, f32[1024,4,128]{2,1,0:T(4,128)} %refs_4_.1, f32[15,256,256]{2,1,0:T(8,128)} %refs_5_.1, ...), custom_call_target="tpu_custom_call" | custom-call | tf_op jit(solution)/shard_map/pallas_call | solution.py:548
  24.1 0.7 %shard_map.87 = (f32[64,1024]{1,0:T(8,128)}, f32[32,64]{1,0:T(8,128)}) custom-call(f32[64,1024]{1,0:T(8,128)S(1)} %get-tuple-element.6.cur_in, bf16[256,128]{1,0:T(8,128)(2,1)S(1)} %get-tuple-element.7.terms_in), custom_call_target="tpu_custom_call" | custom-call | tf_op jit(solution)/shard_map/pallas_call | solution.py:566

commit v8 on v7

--- a/solution.py
+++ b/solution.py
@@ -106,9 +106,10 @@
     for k in range(1, OCTET):
         pl.semaphore_signal(barrier, inc=1, device_id=flip(k), device_id_type=MESH)
     test_load = load(r.test_h, r.gath.at[:, own_rows], r.load_sem.at[1])
-    train_load = load(r.train_h, r.train.at[0], r.load_sem.at[2])
     for i in range(1, 2 * LEVELS):
         load_side(i)
+        if i == 2:
+            train_load = load(r.train_h, r.train.at[0], r.load_sem.at[2])
     piv_load = load(r.piv_h, r.piv, r.load_sem.at[3])
     odds, heaps = [], []
     for level in range(1, LEVELS + 1):
@@ -208,8 +209,8 @@
                 far = value if far is None else far + value
         sums[level] = (near, far)
 
-    def solve(level):
-        size, count = group_of(n_dev, level)
+    def solved(level):
+        _, count = group_of(n_dev, level)
         lev = level - 1
         near, far = sums[level]
         cols = near.shape[0]
@@ -221,7 +222,13 @@
         taken = pl.ds(pl.multiple_of(odd * rank, rank), rank) if kids == 1 else pl.ds(0, 2 * rank)
         cap_high, cap_low = r.caps[0, lev, taken], r.caps[1, lev, taken]
         result = dot_nt(moved.astype(bf16), cap_high)
-        result = result[:cols] + result[cols:] + dot_nt(moved[:cols].astype(bf16), cap_low)
+        return result[:cols] + result[cols:] + dot_nt(moved[:cols].astype(bf16), cap_low)
+
+    def give(level, result):
+        size, count = group_of(n_dev, level)
+        lev = level - 1
+        odd = odds[lev]
+        kids = 1 if count > 1 else 2
         share, out = getattr(r, f"share{level}"), getattr(r, f"out{level}")
         for kid in range(kids):
             out[kid] = packed(result[:, kid * rank : (kid + 1) * rank], level)
@@ -306,6 +313,7 @@
     r.stack[pl.ds(0, width)] = high
     r.stack[pl.ds(width, width)] = low
     gram(1)
+    turn(0)
     test_load.wait()
     pl.semaphore_wait(barrier, octets - 1 + OCTET - 1)
     first_send(1)
@@ -316,7 +324,6 @@
         return carry
 
     lax.fori_loop(1, octets, spread, 0)
-    turn(0)
     gram(2)
     first_send(2)
     train_load.wait()
@@ -333,24 +340,26 @@
     for lev in range(LEVELS):
         prepare(lev)
     first_take(1)
-    first_take(2)
     drain(r.gath.at[:, pl.ds(0, (octets - 1) * half)], r.ag_recv)
     seat_test = r.gath.at[:, seat_rows]
     for k in range(2, OCTET, 2):
         remote(seat_test, seat_test, r.all_send, r.fw_recv, flip(k))
+    first_take(2)
     first_take(3)
     if group_of(n_dev, 3)[1] == 1:
-        solve(3)
+        give(3, solved(3))
     first_take(4)
     if group_of(n_dev, 4)[1] == 1:
-        solve(4)
+        give(4, solved(4))
+    late = [level for level in range(1, LEVELS + 1) if group_of(n_dev, level)[1] > 1]
+    for level in late:
+        second_take(level)
+    results = [solved(level) for level in late]
+    for level, result in zip(late, results):
+        give(level, result)
     drain(r.train.at[0], r.tr_recv)
     widen_train(1)
     turn(LEVELS - 1)
-    for level in (4, 3, 2, 1):
-        if group_of(n_dev, level)[1] > 1:
-            second_take(level)
-            solve(level)
     drain(r.gath.at[:, pl.ds(0, (OCTET // 2 - 1) * octets * half)], r.fw_recv)
     widen_tests()
     fill(0)
@@ -389,13 +398,13 @@
     product = dot(jnp.concatenate([high, low], axis=0), second[1])
     upper = jnp.concatenate([first, second[0] - (product[:width] + product[width:])], axis=1)
     high, low = split(upper)
-    product = dot(jnp.concatenate([high, low], axis=0), r.leff[0])
-    current = r.cur0[...] - (product[:width] + product[width:] + dot(high, r.leff[1]))
-    r.cur[...] = current
-    weights = current.astype(bf16)
+    both = jnp.concatenate([high, low], axis=0)
     for h in range(2):
-        r.wt[0, h] = weights[:, h * (points // 2) : (h + 1) * (points // 2)]
-    for h in range(2):
+        cut = pl.ds(h * (points // 2), points // 2)
+        product = dot(both, r.leff[0, :, cut])
+        current = r.cur0[:, cut] - (product[:width] + product[width:] + dot(high, r.leff[1, :, cut]))
+        r.cur[:, cut] = current
+        r.wt[0, h] = current.astype(bf16)
         remote(r.wt.at[0, h], r.wt.at[1, h], r.all_send, r.wt_recv.at[h], flip(1))
     cur_copy = pltpu.make_async_copy(r.cur, r.cur_out, r.out_sem)
     cur_copy.start()

time: 24.9 us -> 24.7 us (level)
  Pallas kernels: 24.2 us -> 23.9 us
where the time goes in v8:
time: 24.7 us; the launch traced here: 24.6 us
  Pallas kernels  23.9 us (97%)
  between operations  0.64 us (3%)
    pallas_call x1, Pallas kernels, body(): pl.pallas_call(functools.partial(kernel, n_dev, narrow, names), out_shape...  23.2 us
    pallas_call x1, Pallas kernels, body(): pl.pallas_call(finish, out_shape=(jax.ShapeDtypeStruct((width, points), f...  0.74 us

profile of v8, /device:TPU:0, one launch (start us, length us, event | category | flops | bytes accessed | tf_op | source)
XLA Modules:
  0.0 24.6 jit_solution(9036004680487784008)
XLA Ops:
  0.6 23.2 %shard_map.86 = (f32[64,1024]{1,0:T(8,128)S(1)}, bf16[256,128]{1,0:T(8,128)(2,1)S(1)}) custom-call(f32[64,1024]{1,0:T(8,128)} %bitcast.3, bf16[1024,128]{1,0:T(8,128)(2,1)} %refs_1_.1, bf16[2,16,128]{2,1,0:T(8,128)(2,1)} %bitcast.4, f32[1024,4,128]{2,1,0:T(4,128)} %refs_3_.1, f32[1024,4,128]{2,1,0:T(4,128)} %refs_4_.1, f32[15,256,256]{2,1,0:T(8,128)} %refs_5_.1, ...), custom_call_target="tpu_custom_call" | custom-call | tf_op jit(solution)/shard_map/pallas_call | solution.py:557
  23.8 0.7 %shard_map.87 = (f32[64,1024]{1,0:T(8,128)}, f32[32,64]{1,0:T(8,128)}) custom-call(f32[64,1024]{1,0:T(8,128)S(1)} %get-tuple-element.6.cur_in, bf16[256,128]{1,0:T(8,128)(2,1)S(1)} %get-tuple-element.7.terms_in), custom_call_target="tpu_custom_call" | custom-call | tf_op jit(solution)/shard_map/pallas_call | solution.py:575

commit v9 on v8

--- a/solution.py
+++ b/solution.py
@@ -159,6 +159,14 @@
         r.ltl[pl.ds(lev * rank, rank)] = low
 
     sums = {}
+    late = [level for level in range(1, LEVELS + 1) if group_of(n_dev, level)[1] > 1]
+    landed_late = []
+
+    def tall_of(level):
+        return getattr(r, f"send{level}").shape[1]
+
+    def late_at(level):
+        return sum(tall_of(other) for other in late if other < level)
 
     def joined(value, level):
         part = width // group_of(n_dev, level)[0]
@@ -242,13 +250,18 @@
 
     def gathered(level):
         size, _ = group_of(n_dev, level)
-        share = getattr(r, f"share{level}")
-        drain(share.at[pl.ds(0, size - 1)], r.p3_recv.at[level - 1])
+        share, base = (r.share_late, late_at(level)) if level in late else (getattr(r, f"share{level}"), 0)
+        if level not in late:
+            drain(share.at[pl.ds(0, size - 1)], r.p3_recv.at[level - 1])
+        elif not landed_late:
+            landed_late.append(level)
+            drain(share.at[pl.ds(0, size - 1)], r.late_recv)
         part, cut = width // size, rank // size
-        top = share[:, pl.ds(0, 2 * part)].astype(f32)
+        top = share[:, pl.ds(base, 2 * part)].astype(f32)
         top = (top[:, :part] + top[:, part:]).reshape(width, rank)
         return [top] + [
-            share[:, pl.ds(2 * part + k * cut, cut)].reshape(rank, rank) for k in range(level - 1)
+            share[:, pl.ds(base + 2 * part + k * cut, cut)].reshape(rank, rank)
+            for k in range(level - 1)
         ]
 
     def prepare(lev):
@@ -351,12 +364,17 @@
     first_take(4)
     if group_of(n_dev, 4)[1] == 1:
         give(4, solved(4))
-    late = [level for level in range(1, LEVELS + 1) if group_of(n_dev, level)[1] > 1]
     for level in late:
         second_take(level)
     results = [solved(level) for level in late]
     for level, result in zip(late, results):
-        give(level, result)
+        r.out_late[pl.ds(late_at(level), tall_of(level))] = packed(result, level)
+    seat_in_group = pos % OCTET
+    for k in far_first(OCTET):
+        remote(
+            r.out_late, r.share_late.at[seat_in_group], r.all_send, r.late_recv, flip(k)
+        )
+    r.share_late[seat_in_group] = r.out_late[...]
     drain(r.train.at[0], r.tr_recv)
     widen_train(1)
     turn(LEVELS - 1)
@@ -534,14 +552,20 @@
         "terms": vmem((pairs * half, 2 * width), f32),
         "term_b": vmem((pairs * half, 2 * width), bf16),
     }
+    tall_late = 0
     for level in range(1, LEVELS + 1):
         size, count = group_of(n_dev, level)
         tall = (2 * width + (level - 1) * rank) // size
-        for name in ("send", "recv", "share"):
+        for name in ("send", "recv") if count > 1 else ("send", "recv", "share"):
             scratch[f"{name}{level}"] = vmem((size, tall, rank), bf16)
-        scratch[f"out{level}"] = vmem((2, tall, rank), bf16)
-        if count > 1:
+        if count == 1:
+            scratch[f"out{level}"] = vmem((2, tall, rank), bf16)
+        else:
+            tall_late += tall
             scratch[f"hop{level}"] = vmem((count, tall, rank), bf16)
+    scratch["out_late"] = vmem((tall_late, rank), bf16)
+    scratch["share_late"] = vmem((OCTET, tall_late, rank), bf16)
+    scratch["late_recv"] = dma
     scratch["load_sem"] = dma((5,))
     scratch["side_sem"] = dma((LEVELS + 1,))
     scratch["wt_recv"] = dma((2,))

time: 24.7 us -> 24.6 us (level)
  no operation moved by 1% of the time
where the time goes in v9:
time: 24.6 us; the launch traced here: 24.5 us
  Pallas kernels  23.9 us (97%)
  between operations  0.64 us (3%)
    pallas_call x1, Pallas kernels, body(): pl.pallas_call(functools.partial(kernel, n_dev, narrow, names), out_shape...  23.1 us
    pallas_call x1, Pallas kernels, body(): pl.pallas_call(finish, out_shape=(jax.ShapeDtypeStruct((width, points), f...  0.74 us

profile of v9, /device:TPU:0, one launch (start us, length us, event | category | flops | bytes accessed | tf_op | source)
XLA Modules:
  0.0 24.5 jit_solution(7944028755171680483)
XLA Ops:
  0.6 23.1 %shard_map.86 = (f32[64,1024]{1,0:T(8,128)S(1)}, bf16[256,128]{1,0:T(8,128)(2,1)S(1)}) custom-call(f32[64,1024]{1,0:T(8,128)} %bitcast.3, bf16[1024,128]{1,0:T(8,128)(2,1)} %refs_1_.1, bf16[2,16,128]{2,1,0:T(8,128)(2,1)} %bitcast.4, f32[1024,4,128]{2,1,0:T(4,128)} %refs_3_.1, f32[1024,4,128]{2,1,0:T(4,128)} %refs_4_.1, f32[15,256,256]{2,1,0:T(8,128)} %refs_5_.1, ...), custom_call_target="tpu_custom_call" | custom-call | tf_op jit(solution)/shard_map/pallas_call | solution.py:581
  23.8 0.7 %shard_map.87 = (f32[64,1024]{1,0:T(8,128)}, f32[32,64]{1,0:T(8,128)}) custom-call(f32[64,1024]{1,0:T(8,128)S(1)} %get-tuple-element.6.cur_in, bf16[256,128]{1,0:T(8,128)(2,1)S(1)} %get-tuple-element.7.terms_in), custom_call_target="tpu_custom_call" | custom-call | tf_op jit(solution)/shard_map/pallas_call | solution.py:599
